TPU v7x, 8 devices: a whole 2x2x1 slice. The times are simulated.
8 devices in a mesh: dp: 1 (over z), tp: 2 (over y), cp: 4 (over x, core).
Axes of the slice: x: 2, y: 2, z: 1, core: 2. Of those that a mesh axis runs over, the one named last changes fastest.
Arguments:
- tokens: bfloat16 [8192, 1536], P(('dp', 'cp', 'tp'))
- norm_attn: bfloat16 [1536], replicated
- norm_mlp: bfloat16 [1536], replicated
- w_query: bfloat16 [1536, 12, 128], P(None, 'tp')
- w_key: bfloat16 [1536, 2, 128], P(None, 'tp')
- w_value: bfloat16 [1536, 2, 128], P(None, 'tp')
- w_out: bfloat16 [12, 128, 1536], P('tp')
- w_gate: bfloat16 [1536, 8960], P(None, 'tp')
- w_up: bfloat16 [1536, 8960], P(None, 'tp')
- w_down: bfloat16 [8960, 1536], P('tp')
Outputs:
- output 1: bfloat16 [8192, 1536], P(('dp', 'cp', 'tp'))
- output 2: bfloat16 [8192, 256], P(('dp', 'cp'), 'tp')
- output 3: bfloat16 [8192, 256], P(('dp', 'cp'), 'tp')
All inputs are finite; a program needn't handle non-finite values.
Results may differ from a plain program's by a relative error of at most 0.0117268.
Values are sent between devices in bfloat16 or wider.
A program may use at most 1 GiB of HBM per device.

v0:
```python
import functools

import jax
import jax.numpy as jnp
from jax import lax
from jax.experimental import pallas as pl
from jax.experimental.pallas import tpu as pltpu
from jax.sharding import PartitionSpec as P

ROPE_BASE = 500000.0
NORM_EPS = 1e-5
MASK_VALUE = -1e30
LOG2E = 1.4426950408889634
VMEM_LIMIT = 60 * 1024 * 1024
Q_ROWS = 256
K_ROWS = 512
MESH = pl.DeviceIdType.MESH
TILE = 128
N_CHUNKS = 9
N_EARLY = 4


def rms_norm(tensor, gain_vec):
    widened = tensor.astype(jnp.float32)
    inv_rms = lax.rsqrt(jnp.mean(widened * widened, axis=-1, keepdims=True) + NORM_EPS)
    return (widened * inv_rms * gain_vec.astype(jnp.float32)).astype(jnp.bfloat16)


def rope_tables(positions, head_dim):
    half_dim = head_dim // 2
    inv_freq = ROPE_BASE ** (-2.0 * jnp.arange(half_dim, dtype=jnp.float32) / head_dim)
    angles = positions.astype(jnp.float32)[:, None] * inv_freq[None, :]
    return jnp.cos(angles), jnp.sin(angles)


def rope_rotate(proj, tables, head_dim):
    cosine, sine_tab = tables
    half_dim = head_dim // 2
    parts = []
    for h in range(proj.shape[1] // head_dim):
        first_half = proj[:, h * head_dim:h * head_dim + half_dim]
        second_half = proj[:, h * head_dim + half_dim:(h + 1) * head_dim]
        parts += [first_half * cosine - second_half * sine_tab, second_half * cosine + first_half * sine_tab]
    return jnp.concatenate(parts, axis=1).astype(jnp.bfloat16)


class Links:
    def __init__(self, weights, recv, send_sems, recv_sems, n_tiles):
        self.y, self.c = lax.axis_index("tp"), lax.axis_index("cp")
        self.peer = {
            "y": {"tp": 1 - self.y},
            "x": {"cp": lax.rem(self.c + 2, 4)},
            "d": {"cp": self.c + 1 - 2 * lax.rem(self.c, 2)},
        }
        self.weights, self.recv, self.send_sems, self.recv_sems = weights, recv, send_sems, recv_sems
        self.n_tiles = n_tiles
        self.started = []

    def barrier(self):
        sem = pltpu.get_barrier_semaphore()
        for name in "yxd":
            pl.semaphore_signal(sem, inc=1, device_id=self.peer[name], device_id_type=MESH)
        pl.semaphore_wait(sem, 3)

    def remote(self, src, dst, ssem, rsem, to):
        return pltpu.make_async_remote_copy(src_ref=src, dst_ref=dst, send_sem=ssem, recv_sem=rsem, device_id=self.peer[to], device_id_type=MESH)

    def chunk(self, stage, j):
        to = "yxdd"[stage]
        copies = []
        for a in range(3):
            if stage == 0:
                tile = jnp.minimum(4 * j + self.c, self.n_tiles - 1)
                sl = pl.ds(pl.multiple_of(tile * TILE, TILE), TILE)
                src = self.weights[a].at[sl, :] if a == 2 else self.weights[a].at[:, sl]
            else:
                src = self.recv[a].at[j, (0, 0, 0, 1)[stage]]
            copies.append(self.remote(src, self.recv[a].at[j, stage], self.send_sems.at[j, stage, a], self.recv_sems.at[j, stage, a], to))
        return copies

    def start(self, stage, j):
        for copy in self.chunk(stage, j):
            copy.start()

    def arrived(self, stage, j):
        for copy in self.chunk(stage, j):
            copy.wait_recv()

    def sent(self, stage, j):
        for copy in self.chunk(stage, j):
            copy.wait_send()


EARLY_FORWARD = ((0, 16), (1, 20), (2, 23))
EARLY_SECOND = ((0, 20), (1, 23))


def attention_kernel(q_ref, kv_ref, wo_ref, w1_ref, w3_ref, w2_ref, o_ref, kc_ref, vc_ref, ro_ref, r1_ref, r3_ref, r2_ref,
                     kv_buf, m_sc, l_sc, acc_sc, send_sems, recv_sems, kv_send, kv_recv, wo_send, wo_recv):
    head_dim = 128
    chunk_len = kv_ref.shape[2]
    heads = q_ref.shape[2] // head_dim
    chains = 2
    per_chain = heads // chains
    rows = per_chain * Q_ROWS
    q_blocks = chunk_len // Q_ROWS
    coef = head_dim ** -0.5 * LOG2E
    net = Links((w1_ref, w3_ref, w2_ref), (r1_ref, r3_ref, r2_ref), send_sems, recv_sems, w1_ref.shape[1] // TILE)
    y, c = net.y, net.c
    core_lower = lax.rem(c + y, 2)
    chip_lower = lax.rem(c // 2 + y, 2)

    def kv_copy(n):
        src, dst, to = ((None, 1, "x"), (None, 2, "d"), (1, 3, "d"), (None, 4, "y"), (4, 5, "x"), (4, 6, "d"), (5, 7, "d"))[n]
        return net.remote(kv_ref if src is None else kv_buf.at[src], kv_buf.at[dst], kv_send.at[n], kv_recv.at[n], to)

    def wo_copy(stage):
        quarter = wo_ref.shape[0] // 4
        src = wo_ref.at[pl.ds(pl.multiple_of(c * quarter, 64), quarter), :] if stage == 0 else ro_ref.at[(0, 0, 0, 1)[stage]]
        return net.remote(src, ro_ref.at[stage], wo_send.at[stage], wo_recv.at[stage], "yxdd"[stage])

    net.barrier()
    kv_copy(3).start()
    kv_copy(0).start()
    kv_copy(1).start()
    wo_copy(0).start()
    net.start(0, 0)
    net.start(0, 1)
    m_sc[...] = jnp.full_like(m_sc, MASK_VALUE)
    l_sc[...] = jnp.zeros_like(l_sc)
    acc_sc[...] = jnp.zeros_like(acc_sc)
    kv_buf[0] = kv_ref[...]
    kv_copy(1).wait_recv()

    def block(q_parts, state, start, slot, head, off, masked):
        k_blk = kv_buf[slot, head, 0, pl.ds(off, K_ROWS), :]
        v_blk = kv_buf[slot, head, 1, pl.ds(off, K_ROWS), :]
        for a in range(chains):
            s = lax.dot_general(q_parts[a], k_blk, (((1,), (1,)), ((), ())), preferred_element_type=jnp.float32)
            if masked:
                q_pos = start + lax.rem(lax.broadcasted_iota(jnp.int32, (rows, K_ROWS), 0), Q_ROWS)
                k_pos = off + lax.broadcasted_iota(jnp.int32, (rows, K_ROWS), 1)
                s = jnp.where(k_pos <= q_pos, s, MASK_VALUE)
            m_prev = m_sc[state, a]
            m_new = jnp.maximum(m_prev, jnp.max(s, axis=1, keepdims=True))
            alpha = jnp.exp2((m_prev - m_new) * coef)
            mc = m_new * coef
            sums = l_sc[state, a] * alpha
            p_tiles = []
            for j in range(K_ROWS // 128):
                p = jnp.exp2(s[:, j * 128:(j + 1) * 128] * coef - mc)
                sums = sums + p
                p_tiles.append(p.astype(jnp.bfloat16))
            l_sc[state, a] = sums
            m_sc[state, a] = m_new
            p_all = jnp.concatenate(p_tiles, axis=1)
            acc_sc[state, a] = acc_sc[state, a] * alpha + jnp.dot(p_all, v_blk, preferred_element_type=jnp.float32)

    def load_q(head, qb):
        sl = pl.ds(pl.multiple_of(qb * Q_ROWS, Q_ROWS), Q_ROWS)
        return [jnp.concatenate([q_ref[head, sl, (a * per_chain + h) * head_dim:(a * per_chain + h + 1) * head_dim] for h in range(per_chain)], axis=0) for a in range(chains)]

    per_pass = 2 * q_blocks
    per_piece = chunk_len // K_ROWS

    def step(s, carry):
        phase = s // per_pass
        head = lax.rem(s, per_pass) // q_blocks
        qb = lax.rem(s, q_blocks)
        state = lax.rem(s, per_pass)

        def at(k, fn):
            pl.when(s == k)(fn)

        @pl.when(s == 5)
        def _():
            kv_copy(0).wait_recv()
            kv_copy(2).start()

        @pl.when(s == 7)
        def _():
            kv_copy(3).wait_recv()
            kv_copy(4).start()
            kv_copy(5).start()

        @pl.when(s == 8)
        def _():
            kv_copy(2).wait_recv()

        @pl.when(s == 11)
        def _():
            wo_copy(0).wait_recv()
            wo_copy(1).start()
            wo_copy(2).start()

        @pl.when(s == 14)
        def _():
            kv_copy(4).wait_recv()
            kv_copy(6).start()

        @pl.when(s == 16)
        def _():
            kv_copy(5).wait_recv()
            kv_copy(6).wait_recv()
            wo_copy(1).wait_recv()
            wo_copy(3).start()

        for j, when in EARLY_FORWARD:
            @pl.when(s == when)
            def _(j=j):
                net.arrived(0, j)
                net.start(1, j)
                net.start(2, j)
                if j + 2 < N_EARLY:
                    net.start(0, j + 2)

        for j, when in EARLY_SECOND:
            @pl.when(s == when)
            def _(j=j):
                net.arrived(1, j)
                net.start(3, j)

        q_parts = load_q(head, qb)
        start = qb * Q_ROWS
        diag = start // K_ROWS
        is_first = (phase == 0).astype(jnp.int32)
        is_last = (phase == 2).astype(jnp.int32)
        is_mid = 1 - is_first - is_last
        count = is_first * (diag + per_piece * core_lower) + is_mid * 2 * per_piece * chip_lower + is_last * 4 * per_piece * y
        kv_head = head + is_last * (1 - 2 * head)

        def inner(i, carry):
            in_core = (i >= diag).astype(jnp.int32)
            idx = i - is_first * in_core * diag
            slot = is_first * 2 * in_core + is_mid * (1 + 2 * (i // per_piece)) + is_last * (4 + i // per_piece)
            off = (is_first * (in_core * lax.rem(idx, per_piece) + (1 - in_core) * i) + (1 - is_first) * lax.rem(i, per_piece)) * K_ROWS
            block(q_parts, state, start, slot, kv_head, pl.multiple_of(off, K_ROWS), False)
            return carry

        lax.fori_loop(0, count, inner, 0)

        @pl.when(phase == 0)
        def _():
            block(q_parts, state, start, 0, head, pl.multiple_of(diag * K_ROWS, K_ROWS), True)

        return carry

    lax.fori_loop(0, 3 * per_pass, step, 0)

    def finish(state, carry):
        head = state // q_blocks
        sl = pl.ds(pl.multiple_of(lax.rem(state, q_blocks) * Q_ROWS, Q_ROWS), Q_ROWS)
        for a in range(chains):
            total = jnp.sum(l_sc[state, a], axis=1, keepdims=True)
            out = (acc_sc[state, a] / total).astype(jnp.bfloat16)
            for h in range(per_chain):
                o_ref[head, sl, (a * per_chain + h) * head_dim:(a * per_chain + h + 1) * head_dim] = out[h * Q_ROWS:(h + 1) * Q_ROWS]
        return carry

    lax.fori_loop(0, per_pass, finish, 0)

    for e in range(2):
        late = c // 2
        owner = (1 - late) * (2 * c + e) + late * (7 - 2 * c - e)
        cross = lax.rem(late + y, 2)
        slot = 4 * cross + 2 * lax.rem(owner + c, 2) + lax.rem(owner // 2 + c // 2, 2)
        kc_ref[e * chunk_len:(e + 1) * chunk_len] = kv_buf[slot, cross, 0]
        vc_ref[e * chunk_len:(e + 1) * chunk_len] = kv_buf[slot, cross, 1]

    wo_copy(2).wait_recv()
    wo_copy(3).wait_recv()
    for n in range(7):
        kv_copy(n).wait_send()
    for n in range(4):
        wo_copy(n).wait_send()
    forwarded = [j for j, _ in EARLY_FORWARD]
    second = [j for j, _ in EARLY_SECOND]
    for j in range(N_EARLY):
        if j not in forwarded:
            net.arrived(0, j)
        net.sent(0, j)
    for j in forwarded:
        if j not in second:
            net.arrived(1, j)
        net.arrived(2, j)
        net.sent(1, j)
        net.sent(2, j)
    for j in second:
        net.arrived(3, j)
        net.sent(3, j)


def attention(q, kv, wo, w1, w3, w2):
    _, rows, width = q.shape
    dim = w1.shape[0]
    states = 2 * rows // Q_ROWS
    m_rows = width // 128 // 2 * Q_ROWS
    vm = pl.BlockSpec(memory_space=pltpu.VMEM)
    hbm = pl.BlockSpec(memory_space=pl.ANY)
    bf16 = jnp.bfloat16
    n = N_EARLY
    return pl.pallas_call(
        attention_kernel,
        in_specs=[vm, vm, hbm, hbm, hbm, hbm],
        out_specs=[vm, vm, vm, hbm, hbm, hbm, hbm],
        out_shape=[
            jax.ShapeDtypeStruct(q.shape, bf16),
            jax.ShapeDtypeStruct((2 * rows, 128), bf16),
            jax.ShapeDtypeStruct((2 * rows, 128), bf16),
            jax.ShapeDtypeStruct((4, wo.shape[0] // 4, dim), bf16),
            jax.ShapeDtypeStruct((N_CHUNKS, 4, dim, TILE), bf16),
            jax.ShapeDtypeStruct((N_CHUNKS, 4, dim, TILE), bf16),
            jax.ShapeDtypeStruct((N_CHUNKS, 4, TILE, dim), bf16),
        ],
        scratch_shapes=[
            pltpu.VMEM((8,) + kv.shape, bf16),
            pltpu.VMEM((states, 2, m_rows, 128), jnp.float32),
            pltpu.VMEM((states, 2, m_rows, 128), jnp.float32),
            pltpu.VMEM((states, 2, m_rows, 128), jnp.float32),
            pltpu.SemaphoreType.DMA((n, 4, 3)),
            pltpu.SemaphoreType.DMA((n, 4, 3)),
            pltpu.SemaphoreType.DMA((7,)),
            pltpu.SemaphoreType.DMA((7,)),
            pltpu.SemaphoreType.DMA((4,)),
            pltpu.SemaphoreType.DMA((4,)),
        ],
        compiler_params=pltpu.CompilerParams(collective_id=0, has_side_effects=True, vmem_limit_bytes=VMEM_LIMIT),
        cost_estimate=pl.CostEstimate(flops=16 * rows * 4096 * width, bytes_accessed=32 * 2**20, transcendentals=rows * 4096 * 12),
        name="attention",
    )(q, kv, wo, w1, w3, w2)


M_BLOCK = 512
LATE_FORWARD = {0: (3,), 4: (4,), 9: (5,)}
LATE_SECOND = {0: (2,), 5: (3,), 10: (4,)}
END_FORWARD = {12: (6,), 14: (7,), 15: (8,)}
END_SECOND = {12: (5,), 14: (6,), 15: (7,), 16: (8,)}
LOAD_AFTER = 12


def mlp_kernel(b_ref, res_ref, w1_ref, w3_ref, w2_ref, a1_ref, a3_ref, a2_ref, out_ref, r1_ref, r3_ref, r2_ref,
               w1_sc, w3_sc, w2_sc, acc_sc, load_sems, send_sems, recv_sems):
    dim = b_ref.shape[1]
    width = 4 * TILE
    n_tiles = w1_ref.shape[1] // TILE
    net = Links((w1_ref, w3_ref, w2_ref), (r1_ref, r3_ref, r2_ref), send_sems, recv_sems, n_tiles)
    own_last = (n_tiles - 4) * TILE

    def own_loads(j, slot):
        off = min(j * width, own_last) if isinstance(j, int) else pl.multiple_of(jnp.minimum(j * width, own_last), TILE)
        sl = pl.ds(off, width)
        return [
            pltpu.make_async_copy(w1_ref.at[:, sl], w1_sc.at[slot], load_sems.at[slot, 0]),
            pltpu.make_async_copy(w3_ref.at[:, sl], w3_sc.at[slot], load_sems.at[slot, 1]),
            pltpu.make_async_copy(w2_ref.at[sl, :], w2_sc.at[slot], load_sems.at[slot, 2]),
        ]

    def other_loads(j, slot):
        copies = []
        for p in range(4):
            sl = pl.ds(p * TILE, TILE)
            copies.append(pltpu.make_async_copy(r1_ref.at[j, p], w1_sc.at[slot, :, sl], load_sems.at[slot, 0]))
            copies.append(pltpu.make_async_copy(r3_ref.at[j, p], w3_sc.at[slot, :, sl], load_sems.at[slot, 1]))
            copies.append(pltpu.make_async_copy(r2_ref.at[j, p], w2_sc.at[slot, sl, :], load_sems.at[slot, 2]))
        return copies

    def compute(slot, lane_keep):
        def rows_step(m, carry):
            sl = pl.ds(pl.multiple_of(m * M_BLOCK, M_BLOCK), M_BLOCK)
            b = b_ref[sl, :]
            gate = jnp.dot(b, w1_sc[slot], preferred_element_type=jnp.float32)
            up = jnp.dot(b, w3_sc[slot], preferred_element_type=jnp.float32)
            hidden = jax.nn.silu(gate) * up
            hidden = jnp.where(lane_keep > 0.5, hidden, 0.0).astype(jnp.bfloat16)
            acc_sc[sl, :] += jnp.dot(hidden, w2_sc[slot], preferred_element_type=jnp.float32)
            return carry

        lax.fori_loop(0, b_ref.shape[0] // M_BLOCK, rows_step, 0)

    net.barrier()
    net.start(0, 4)
    net.start(0, 5)
    for copy in own_loads(0, 0):
        copy.start()
    acc_sc[...] = res_ref[...].astype(jnp.float32)
    lane_tile = lax.broadcasted_iota(jnp.int32, (1, width), 1) // TILE
    source = 2 * lax.rem(lane_tile + net.c // 2, 2) + lax.rem(lane_tile // 2 + lax.rem(net.c, 2), 2)

    def pass_on(s, forward, second):
        for when, chunks in forward.items():
            @pl.when(s == when)
            def _(chunks=chunks):
                for j in chunks:
                    if j >= N_EARLY:
                        net.arrived(0, j)
                    net.start(1, j)
                    net.start(2, j)
                    if 6 <= j + 2 < N_CHUNKS:
                        net.start(0, j + 2)
        for when, chunks in second.items():
            @pl.when(s == when)
            def _(chunks=chunks):
                for j in chunks:
                    if j >= 3:
                        net.arrived(1, j)
                    net.start(3, j)

    def load_next(s, slot, after):
        for j in range(2, N_CHUNKS):
            if (N_CHUNKS - 1 + j >= LOAD_AFTER) == after:
                @pl.when(s == N_CHUNKS - 1 + j)
                def _(j=j):
                    if j >= 3:
                        net.arrived(2, j)
                    net.arrived(3, j)

        if not after:
            @pl.when(s + 1 < N_CHUNKS)
            def _():
                for copy in own_loads(s + 1, 1 - slot):
                    copy.start()

        first, last = (LOAD_AFTER, 2 * N_CHUNKS - 1) if after else (N_CHUNKS - 1, LOAD_AFTER)

        @pl.when((s >= first) & (s < last))
        def _():
            for copy in other_loads(s + 1 - N_CHUNKS, 1 - slot):
                copy.start()

    def step(s, carry):
        slot = lax.rem(s, 2)
        pass_on(s, LATE_FORWARD, LATE_SECOND)
        load_next(s, slot, False)
        for copy in own_loads(0, slot):
            copy.wait()
        own_end = (s == N_CHUNKS - 1).astype(jnp.float32)
        other_end = (s == 2 * N_CHUNKS - 1).astype(jnp.float32)
        keep = 1.0 - own_end * (lane_tile == 0).astype(jnp.float32) - other_end * (source == 3).astype(jnp.float32)
        compute(slot, keep)
        pass_on(s, END_FORWARD, END_SECOND)
        load_next(s, slot, True)
        return carry

    lax.fori_loop(0, 2 * N_CHUNKS, step, 0)
    out_ref[...] = acc_sc[...].astype(out_ref.dtype)
    for j in range(4, N_CHUNKS):
        net.sent(0, j)
    for j in range(3, N_CHUNKS):
        net.sent(1, j)
        net.sent(2, j)
    for j in range(2, N_CHUNKS):
        net.sent(3, j)


def mlp(b, res, w1, w3, w2, early):
    rows, dim = b.shape
    vm = pl.BlockSpec(memory_space=pltpu.VMEM)
    hbm = pl.BlockSpec(memory_space=pl.ANY)
    bf16 = jnp.bfloat16
    width = 4 * TILE
    n = N_CHUNKS
    return pl.pallas_call(
        mlp_kernel,
        in_specs=[vm, vm] + [hbm] * 6,
        out_specs=[vm, hbm, hbm, hbm],
        out_shape=[jax.ShapeDtypeStruct((rows, dim), bf16)] + [jax.ShapeDtypeStruct(a.shape, bf16) for a in early],
        input_output_aliases={5: 1, 6: 2, 7: 3},
        scratch_shapes=[
            pltpu.VMEM((2, dim, width), bf16),
            pltpu.VMEM((2, dim, width), bf16),
            pltpu.VMEM((2, width, dim), bf16),
            pltpu.VMEM((rows, dim), jnp.float32),
            pltpu.SemaphoreType.DMA((2, 3)),
            pltpu.SemaphoreType.DMA((n, 4, 3)),
            pltpu.SemaphoreType.DMA((n, 4, 3)),
        ],
        compiler_params=pltpu.CompilerParams(collective_id=1, has_side_effects=True, vmem_limit_bytes=VMEM_LIMIT),
        cost_estimate=pl.CostEstimate(flops=12 * rows * dim * w1.shape[1], bytes_accessed=12 * dim * w1.shape[1], transcendentals=2 * rows * w1.shape[1]),
        name="mlp",
    )(b, res, w1, w3, w2, *early)[0]

def solution(mesh):
    cp_size = mesh.shape["cp"]
    tp_swap = [(0, 1), (1, 0)]
    chip_swap = [(0, 2), (2, 0), (1, 3), (3, 1)]
    core_swap = [(0, 1), (1, 0), (2, 3), (3, 2)]

    def swap_tp(a):
        return lax.ppermute(a, "tp", tp_swap)

    def swap_chip(a):
        return lax.ppermute(a, "cp", chip_swap)

    def swap_core(a):
        return lax.ppermute(a, "cp", core_swap)

    def spread(a):
        b = swap_chip(a)
        return [a, b, swap_core(a), swap_core(b)]

    def layer_shard(x_loc, norm_attn, norm_mlp, w_query, w_key, w_value, w_out, w_gate, w_up, w_down):
        tok_dev, dim = x_loc.shape
        local_q, head_dim = w_query.shape[1], w_query.shape[2]
        cp_index = lax.axis_index("cp")
        tp_index = lax.axis_index("tp")
        n_pieces = 2 * cp_size
        piece = jnp.where(tp_index == 0, cp_index, n_pieces - 1 - cp_index)
        tables = rope_tables(piece * tok_dev + jnp.arange(tok_dev, dtype=jnp.int32), head_dim)

        peers = jnp.arange(cp_size, dtype=jnp.int32) ^ cp_index
        rel_slot = jnp.where(peers == 1, 2, jnp.where(peers == 2, 1, peers))

        wq = w_query.reshape(dim, local_q * head_dim)
        wkv = jnp.concatenate([w_key.reshape(dim, -1), w_value.reshape(dim, -1)], axis=1)
        wo = w_out.reshape(local_q * head_dim, dim)

        def other_half_rows(w):
            quarter = w.shape[0] // cp_size
            own = lax.dynamic_slice_in_dim(w, cp_index * quarter, quarter, axis=0)
            stack = jnp.stack(spread(swap_tp(own)))
            return jnp.take(stack, rel_slot, axis=0).reshape(w.shape)

        wkv_other = other_half_rows(wkv)
        wq_other = other_half_rows(wq)

        normed = rms_norm(x_loc, norm_attn)
        dot = functools.partial(jnp.dot, preferred_element_type=jnp.float32)

        def kv_pair(w):
            proj = dot(normed, w)
            return jnp.stack([rope_rotate(proj[:, :head_dim], tables, head_dim), proj[:, head_dim:].astype(jnp.bfloat16)])

        kv = jnp.stack([kv_pair(wkv), kv_pair(wkv_other)])
        q = jnp.stack([rope_rotate(dot(normed, wq), tables, head_dim), rope_rotate(dot(normed, wq_other), tables, head_dim)])
        o, k_cache, v_cache, wo_parts, *early = attention(q, kv, wo, w_gate, w_up, w_down)
        wo_other = jnp.take(wo_parts, rel_slot, axis=0).reshape(wo.shape)
        residual = (x_loc.astype(jnp.float32) + (dot(o[0], wo) + dot(o[1], wo_other))).astype(jnp.bfloat16)
        layer_out = mlp(rms_norm(residual, norm_mlp), residual, w_gate, w_up, w_down, early)
        return layer_out, k_cache, v_cache

    row_spec = P(("dp", "cp", "tp"), None)
    cache_spec = P(("dp", "cp"), "tp")
    head_spec = P(None, "tp", None)
    return jax.shard_map(
        layer_shard,
        mesh=mesh,
        in_specs=(row_spec, P(None), P(None), head_spec, head_spec, head_spec, P("tp", None, None), P(None, "tp"), P(None, "tp"), P("tp", None)),
        out_specs=(row_spec, cache_spec, cache_spec),
        check_vma=False,
    )
```

profile of v0, /device:TPU:5, one launch (start us, length us, event | category | flops | bytes accessed | tf_op | source)
XLA Modules:
  0.0 457.6 jit_solution(17246714363969365794)
XLA Ops:
  0.6 1.6 fusion.155
  2.3 0.0 collective-permute-start.4
  2.3 2.8 copy.77
  5.1 0.0 copy-start.1
  5.1 0.0 copy-start.15
  5.1 0.0 copy-start.2
  5.2 0.0 copy-start.13
  5.2 0.0 copy-start.14
  5.2 0.9 constant_dynamic-slice_fusion
  6.1 1.5 collective-permute-start
  7.5 2.6 fusion.3
  10.2 2.0 fusion.12
  12.2 4.3 fusion.163
  16.6 3.7 fusion.143
  20.2 3.2 fusion.144
  23.5 0.1 broadcast_in_dim.48
  23.6 4.8 %concatenate.115 = bf16[1,1024,768]{2,1,0:T(8,128)(2,1)} concatenate(bf16[1,1024,64]{2,1,0:T(8,128)(2,1)} %get-tuple-element.29, bf16[1,1024,64]{2,1,0:T(8,128)(2,1)} %get-tuple-element.30, bf16[1,1024,64]{2,1,0:T(8,128)(2,1)} %get-tuple-element.26, bf16[1,1024,64]{2,1,0:T(8,128)(2,1)} %get-tuple-element.28, bf16[1,1024,64]{2,1,0:T(8,128)(2,1)} %get-tuple-element.24, ...), dimensions={2} | concatenate | bytes 3145728 | tf_op jit(solution)/shard_map/concatenate | solution.py:44
  28.4 0.0 collective-permute-done.4
  28.4 1.3 collective-permute-start.5
  29.8 1.5 collective-permute-start.6
  31.2 2.4 collective-permute-done.5
  33.7 2.1 collective-permute-start.7
  35.8 1.8 fusion.125
  37.5 0.0 collective-permute-done
  37.5 1.3 collective-permute-start.1
  38.8 0.0 collective-permute-done.6
  38.8 0.0 collective-permute-done.7
  38.8 1.9 pad_maximum_fusion.5
  40.7 2.6 gather_fusion.1
  43.4 0.3 collective-permute-start.2
  43.6 1.4 bitcast_select_fusion.1
  45.1 7.5 %collective-permute-done.1 = bf16[384,768]{0,1:T(8,128)(2,1)} collective-permute-done((bf16[384,768]{0,1:T(8,128)(2,1)}, bf16[384,768]{0,1:T(8,128)(2,1)}, u32[]{:S(2)}, u32[]{:S(2)}) %collective-permute-start.1) | collective-permute-done | bytes 589856 | tf_op jit(solution)/shard_map/ppermute | solution.py:492
  52.5 0.8 collective-permute-start.3
  53.3 1.0 fusion.158
  54.3 0.0 copy-start.8
  54.4 0.0 collective-permute-done.2
  54.4 0.5 collective-permute-done.3
  54.9 0.4 copy-done.8
  55.3 1.6 pad_maximum_fusion.1
  56.9 2.3 gather_fusion
  59.2 2.8 copy.90
  62.0 0.0 copy-start.4
  62.0 0.4 bitcast_select_fusion
  62.5 1.4 copy-done.4
  63.9 2.7 fusion.161
  66.6 3.5 fusion.130
  70.2 3.9 fusion.131
  74.1 0.0 copy-done.10
  74.1 0.3 maximum_bitcast_fusion
  74.4 1.1 pad_maximum_fusion.2.kv_ref
  75.5 4.1 concatenate.128
  79.6 1.9 pad_maximum_fusion.q_ref
  81.5 173.7 %attention.1 = (bf16[2,1024,768]{2,1,0:T(8,128)(2,1)}, bf16[2048,128]{1,0:T(8,128)(2,1)}, bf16[2048,128]{1,0:T(8,128)(2,1)}, bf16[4,192,1536]{2,1,0:T(8,128)(2,1...) custom-call(bf16[2,1024,768]{2,1,0:T(8,128)(2,1)} %pad_maximum_fusion.q_r, ...), custom_call_target="tpu_custom_call" | custom-call | flops 51539607552 | bytes 33554432 | tf_op jit(solution)/shard_map/attention/pallas_call | solution.py:302
  255.2 2.4 gather_fusion.2
  257.5 0.0 copy-start.17
  257.5 0.3 broadcast_select_fusion
  257.8 1.4 copy-done.17
  259.2 4.2 fusion.8
  263.4 3.2 fusion
  266.6 2.7 fusion.2.b_ref
  269.3 182.9 %mlp.1 = (bf16[1024,1536]{1,0:T(8,128)(2,1)}, bf16[9,4,1536,128]{3,2,1,0:T(8,128)(2,1)}, bf16[9,4,1536,128]{3,2,1,0:T(8,128)(2,1)}, bf16[9,4,128,1536]{3,2,1,0:T(8,128)(2,1)}) custom-call(bf16[1024,1536]{1,0:T(8,128)(2,1)} %fusion.2.b_ref, bf16[1024,1536]{1,0:T(8,128)(2,1)} %copy-done.6, ...), custom_call_target="tpu_custom_call", output_to_operand_aliasing={{1}: (5, {}), {2}: (6, {}), {3}: (7, {})} | custom-call | flops 84557168640 | bytes 82575360 | tf_op jit(solution)/shard_map/mlp/pallas_call | solution.py:462
  452.2 3.8 copy.119
  456.0 0.8 copy.120
  456.8 0.8 copy.121
  (37 shorter events, 0.2 us)
Async XLA Ops:
  2.3 26.1 %collective-permute-start.4 = (bf16[384,256]{1,0:T(8,128)(2,1)}, bf16[384,256]{1,0:T(8,128)(2,1)}, u32[]{:S(2)}, u32[]{:S(2)}) collective-permute-start(bf16[384,256]{1,0:T(8,128)(2,1)} %fusion.155), channel_id=1, source_target_pairs={{0,4},{4,0},{1,5},{5,1},{2,6},{6,2},{3,7},{7,3}} | collective-permute-start | bytes 589832 | tf_op jit(solution)/shard_map/ppermute | solution.py:489
  5.1 5.0 %copy-start.1 = (bf16[1536,6,128]{0,2,1:T(8,128)(2,1)}, bf16[1536,6,128]{0,2,1:T(8,128)(2,1)S(1)}, u32[]{:S(2)}) copy-start(bf16[1536,6,128]{0,2,1:T(8,128)(2,1)S(1)} %copy.77) | copy-start | bytes 7077892
  5.1 5.0 %copy-start.15 = (bf16[1536]{0:T(1024)(128)(2,1)S(1)}, bf16[1536]{0:T(1024)(128)(2,1)}, u32[]{:S(2)}) copy-start(bf16[1536]{0:T(1024)(128)(2,1)} %param.11) | copy-start | bytes 9220
  5.1 5.0 %copy-start.2 = (bf16[1024,1536]{1,0:T(8,128)(2,1)S(1)}, bf16[1024,1536]{1,0:T(8,128)(2,1)}, u32[]{:S(2)}) copy-start(bf16[1024,1536]{1,0:T(8,128)(2,1)} %param.10) | copy-start | bytes 9437188
  5.2 5.0 %copy-start.13 = (bf16[1536,1,128]{2,0,1:T(8,128)(2,1)S(1)}, bf16[1536,1,128]{2,0,1:T(8,128)(2,1)}, u32[]{:S(2)}) copy-start(bf16[1536,1,128]{2,0,1:T(8,128)(2,1)} %param.15) | copy-start | bytes 1179652
  5.2 5.0 %copy-start.14 = (bf16[1536,1,128]{2,0,1:T(8,128)(2,1)S(1)}, bf16[1536,1,128]{2,0,1:T(8,128)(2,1)}, u32[]{:S(2)}) copy-start(bf16[1536,1,128]{2,0,1:T(8,128)(2,1)} %param.14) | copy-start | bytes 1179652
  6.1 31.5 %collective-permute-start = (bf16[384,768]{0,1:T(8,128)(2,1)}, bf16[384,768]{0,1:T(8,128)(2,1)}, u32[]{:S(2)}, u32[]{:S(2)}) collective-permute-start(bf16[384,768]{0,1:T(8,128)(2,1)} %constant_dynamic-slice_fusion), channel_id=1, source_target_pairs={{0,4},{4,0},{1,5},{5,1},{2,6},{6,2},{3,7},{7,3}} | collective-permute-start | bytes 1769480 | tf_op jit(solution)/shard_map/ppermute | solution.py:489
  20.2 3.3 copy-start.16
  28.4 24.9 %copy-start.3 = (bf16[1024,1536]{1,0:T(8,128)(2,1)S(1)}, bf16[1024,1536]{1,0:T(8,128)(2,1)}, u32[]{:S(2)}) copy-start(bf16[1024,1536]{1,0:T(8,128)(2,1)} %param.10) | copy-start | bytes 9437188
  28.4 5.2 %collective-permute-start.5 = (bf16[384,256]{1,0:T(8,128)(2,1)}, bf16[384,256]{1,0:T(8,128)(2,1)S(1)}, u32[]{:S(2)}, u32[]{:S(2)}) collective-permute-start(bf16[384,256]{1,0:T(8,128)(2,1)} %collective-permute-done.4), channel_id=1, source_target_pairs={{0,2},{2,0},{1,3},{3,1},{4,6},{6,4},{5,7},{7,5}} | collective-permute-start | bytes 589832 | tf_op jit(solution)/shard_map/ppermute | solution.py:492
  29.8 9.1 %collective-permute-start.6 = (bf16[384,256]{1,0:T(8,128)(2,1)}, bf16[384,256]{1,0:T(8,128)(2,1)S(1)}, u32[]{:S(2)}, u32[]{:S(2)}) collective-permute-start(bf16[384,256]{1,0:T(8,128)(2,1)} %collective-permute-done.4), channel_id=1, source_target_pairs={{0,1},{1,0},{2,3},{3,2},{4,5},{5,4},{6,7},{7,6}} | collective-permute-start | bytes 589832 | tf_op jit(solution)/shard_map/ppermute | solution.py:495
  33.7 5.2 %collective-permute-start.7 = (bf16[384,256]{1,0:T(8,128)(2,1)S(1)}, bf16[384,256]{1,0:T(8,128)(2,1)S(1)}, u32[]{:S(2)}, u32[]{:S(2)}) collective-permute-start(bf16[384,256]{1,0:T(8,128)(2,1)S(1)} %collective-permute-done.5), channel_id=1, source_target_pairs={{0,1},{1,0},{2,3},{3,2},{4,5},{5,4},{6,7},{7,6}} | collective-permute-start | bytes 589832 | tf_op jit(solution)/shard_map/ppermute | solution.py:495
  37.5 15.0 %collective-permute-start.1 = (bf16[384,768]{0,1:T(8,128)(2,1)}, bf16[384,768]{0,1:T(8,128)(2,1)}, u32[]{:S(2)}, u32[]{:S(2)}) collective-permute-start(bf16[384,768]{0,1:T(8,128)(2,1)} %collective-permute-done), channel_id=1, source_target_pairs={{0,2},{2,0},{1,3},{3,1},{4,6},{6,4},{5,7},{7,5}} | collective-permute-start | bytes 1769480 | tf_op jit(solution)/shard_map/ppermute | solution.py:492
  43.4 11.0 %collective-permute-start.2 = (bf16[384,768]{0,1:T(8,128)(2,1)}, bf16[384,768]{0,1:T(8,128)(2,1)S(1)}, u32[]{:S(2)}, u32[]{:S(2)}) collective-permute-start(bf16[384,768]{0,1:T(8,128)(2,1)} %collective-permute-done), channel_id=1, source_target_pairs={{0,1},{1,0},{2,3},{3,2},{4,5},{5,4},{6,7},{7,6}} | collective-permute-start | bytes 1769480 | tf_op jit(solution)/shard_map/ppermute | solution.py:495
  52.5 2.4 collective-permute-start.3
  54.3 1.0 copy-start.8
  62.0 1.9 copy-start.4
  63.9 2.7 copy-start.7
  63.9 2.7 copy-start.9
  70.2 3.9 copy-start.10
  74.4 5.2 %copy-start = (bf16[1,1024,768]{2,1,0:T(8,128)(2,1)S(1)}, bf16[1,1024,768]{2,1,0:T(8,128)(2,1)}, u32[]{:S(2)}) copy-start(bf16[1,1024,768]{2,1,0:T(8,128)(2,1)} %concatenate.115) | copy-start | bytes 4718596
  257.5 1.7 copy-start.17
  259.2 4.2 copy-start.5
  259.2 4.2 copy-start.18
  266.6 2.7 copy-start.6
  452.2 3.9 copy-start.12
  452.2 4.7 %copy-start.11 = (bf16[2048,128]{1,0:T(8,128)(2,1)S(1)}, bf16[2048,128]{1,0:T(8,128)(2,1)}, u32[]{:S(2)}) copy-start(bf16[2048,128]{1,0:T(8,128)(2,1)} %get-tuple-element.62) | copy-start | bytes 1572868
where the time goes:
time: 463 us; the launch traced here: 458 us
  Pallas kernels  357 us (77%)
  local copies, waits for them, and re-layouts  33.3 us (7%)
  other arithmetic  30.3 us (7%)
  matrix products  17.4 us (4%)
  waiting for transfers between devices  10.4 us (2%)
  starting transfers between devices  8.68 us (2%)
    pallas_call x1, Pallas kernels, mlp(): pl.pallas_call(mlp_kernel, in_specs=[vm, vm] + [hbm] * 6, out_specs=[vm,...  183 us
    pallas_call x1, Pallas kernels, attention(): pl.pallas_call(attention_kernel, in_specs=[vm, vm, hbm, hbm, hbm, hbm], o...  174 us
    concatenate x4, other arithmetic, rope_rotate(): return jnp.concatenate(parts, axis=1).astype(jnp.bfloat16)  14.3 us
    unnamed x42, local copies, waits for them, and re-layouts  11.5 us
    ppermute x2, waiting for transfers between devices, swap_chip(): return lax.ppermute(a, 'cp', chip_swap)  9.91 us
  transfers between devices with their start and end apart: 8, of which 3 were waited for; matrix products, arithmetic and copies ran while one was open for 7% of the time, Pallas kernels for 0%

commit v1 on v0

--- a/solution.py
+++ b/solution.py
@@ -17,13 +17,7 @@
 MESH = pl.DeviceIdType.MESH
 TILE = 128
 N_CHUNKS = 9
-N_EARLY = 4
-
-
-def rms_norm(tensor, gain_vec):
-    widened = tensor.astype(jnp.float32)
-    inv_rms = lax.rsqrt(jnp.mean(widened * widened, axis=-1, keepdims=True) + NORM_EPS)
-    return (widened * inv_rms * gain_vec.astype(jnp.float32)).astype(jnp.bfloat16)
+N_EARLY = 5
 
 
 def rope_tables(positions, head_dim):
@@ -31,17 +25,6 @@
     inv_freq = ROPE_BASE ** (-2.0 * jnp.arange(half_dim, dtype=jnp.float32) / head_dim)
     angles = positions.astype(jnp.float32)[:, None] * inv_freq[None, :]
     return jnp.cos(angles), jnp.sin(angles)
-
-
-def rope_rotate(proj, tables, head_dim):
-    cosine, sine_tab = tables
-    half_dim = head_dim // 2
-    parts = []
-    for h in range(proj.shape[1] // head_dim):
-        first_half = proj[:, h * head_dim:h * head_dim + half_dim]
-        second_half = proj[:, h * head_dim + half_dim:(h + 1) * head_dim]
-        parts += [first_half * cosine - second_half * sine_tab, second_half * cosine + first_half * sine_tab]
-    return jnp.concatenate(parts, axis=1).astype(jnp.bfloat16)
 
 
 class Links:
@@ -91,15 +74,24 @@
             copy.wait_send()
 
 
-EARLY_FORWARD = ((0, 16), (1, 20), (2, 23))
-EARLY_SECOND = ((0, 20), (1, 23))
-
-
-def attention_kernel(q_ref, kv_ref, wo_ref, w1_ref, w3_ref, w2_ref, o_ref, kc_ref, vc_ref, ro_ref, r1_ref, r3_ref, r2_ref,
-                     kv_buf, m_sc, l_sc, acc_sc, send_sems, recv_sems, kv_send, kv_recv, wo_send, wo_recv):
+EARLY_FORWARD = ((0, 14), (1, 17), (2, 19), (3, 21))
+EARLY_SECOND = ((0, 18), (1, 20), (2, 22))
+SLOT_SOURCE = (0, 0, 0, 1)
+
+
+def normed_rows(wide, gain):
+    inv_rms = lax.rsqrt(jnp.mean(wide * wide, axis=-1, keepdims=True) + NORM_EPS)
+    return (wide * inv_rms * gain).astype(jnp.bfloat16)
+
+
+def attention_kernel(x_ref, gain_ref, cos_ref, sin_ref, wq_ref, wkv_ref, wo_ref, w1_ref, w3_ref, w2_ref,
+                     o_ref, kc_ref, vc_ref, ro_ref, r1_ref, r3_ref, r2_ref,
+                     a_sc, q_sc, wq_sc, wkv_sc, kv_buf, m_sc, l_sc, acc_sc, send_sems, recv_sems, kv_send, kv_recv, wt_send, wt_recv):
     head_dim = 128
-    chunk_len = kv_ref.shape[2]
-    heads = q_ref.shape[2] // head_dim
+    half_dim = head_dim // 2
+    chunk_len = x_ref.shape[0]
+    width = wq_ref.shape[1]
+    heads = width // head_dim
     chains = 2
     per_chain = heads // chains
     rows = per_chain * Q_ROWS
@@ -109,28 +101,66 @@
     y, c = net.y, net.c
     core_lower = lax.rem(c + y, 2)
     chip_lower = lax.rem(c // 2 + y, 2)
-
-    def kv_copy(n):
-        src, dst, to = ((None, 1, "x"), (None, 2, "d"), (1, 3, "d"), (None, 4, "y"), (4, 5, "x"), (4, 6, "d"), (5, 7, "d"))[n]
-        return net.remote(kv_ref if src is None else kv_buf.at[src], kv_buf.at[dst], kv_send.at[n], kv_recv.at[n], to)
-
-    def wo_copy(stage):
-        quarter = wo_ref.shape[0] // 4
-        src = wo_ref.at[pl.ds(pl.multiple_of(c * quarter, 64), quarter), :] if stage == 0 else ro_ref.at[(0, 0, 0, 1)[stage]]
-        return net.remote(src, ro_ref.at[stage], wo_send.at[stage], wo_recv.at[stage], "yxdd"[stage])
+    other_chip = lax.rem(c + 2, 4)
+
+    def kv_copy(n, hd):
+        src, dst, to = ((0, 1, "x"), (0, 2, "d"), (1, 3, "d"), (0, 4, "y"), (4, 5, "x"), (4, 6, "d"), (5, 7, "d"))[n]
+        return net.remote(kv_buf.at[src, hd], kv_buf.at[dst, hd], kv_send.at[n, hd], kv_recv.at[n, hd], to)
+
+    def weight_copy(kind, stage):
+        own, held = ((wkv_ref, wkv_sc), (wq_ref, wq_sc), (wo_ref, ro_ref))[kind]
+        quarter = own.shape[0] // 4
+        sl = pl.ds(pl.multiple_of((other_chip if stage == 3 else c) * quarter, 64), quarter)
+        src = own if stage == 0 else held
+        return net.remote(src.at[sl, :], held.at[sl, :], wt_send.at[kind, stage], wt_recv.at[kind, stage], "yxdd"[stage])
+
+    def row_slice(i):
+        return pl.ds(pl.multiple_of(i * Q_ROWS, Q_ROWS), Q_ROWS)
+
+    def rope(t, sl):
+        return (t * cos_ref[sl, :] + pltpu.roll(t, half_dim, 1) * sin_ref[sl, :]).astype(jnp.bfloat16)
+
+    def norm_x():
+        def body(i, carry):
+            sl = row_slice(i)
+            a_sc[sl, :] = normed_rows(x_ref[sl, :].astype(jnp.float32), gain_ref[...].astype(jnp.float32))
+            return carry
+        lax.fori_loop(0, q_blocks, body, 0)
+
+    def make_kv(w_ref, hd):
+        def body(i, carry):
+            sl = row_slice(i)
+            proj = jnp.dot(a_sc[sl, :], w_ref[...], preferred_element_type=jnp.float32)
+            kv_buf[0, hd, 0, sl, :] = rope(proj[:, :head_dim], sl)
+            kv_buf[0, hd, 1, sl, :] = proj[:, head_dim:].astype(jnp.bfloat16)
+            return carry
+        lax.fori_loop(0, q_blocks, body, 0)
+
+    def make_q(w_ref, hd):
+        def body(i, carry):
+            sl = row_slice(i)
+            proj = jnp.dot(a_sc[sl, :], w_ref[...], preferred_element_type=jnp.float32)
+            for h in range(heads):
+                cols = slice(h * head_dim, (h + 1) * head_dim)
+                q_sc[hd, sl, cols] = rope(proj[:, cols], sl)
+            return carry
+        lax.fori_loop(0, q_blocks, body, 0)
 
     net.barrier()
-    kv_copy(3).start()
-    kv_copy(0).start()
-    kv_copy(1).start()
-    wo_copy(0).start()
-    net.start(0, 0)
-    net.start(0, 1)
+    weight_copy(0, 0).start()
+    weight_copy(1, 0).start()
+    norm_x()
+    make_kv(wkv_ref, 0)
     m_sc[...] = jnp.full_like(m_sc, MASK_VALUE)
     l_sc[...] = jnp.zeros_like(l_sc)
     acc_sc[...] = jnp.zeros_like(acc_sc)
-    kv_buf[0] = kv_ref[...]
-    kv_copy(1).wait_recv()
+    weight_copy(0, 0).wait_recv()
+    weight_copy(0, 1).start()
+    weight_copy(0, 2).start()
+    kv_copy(1, 0).start()
+    kv_copy(0, 0).start()
+    kv_copy(3, 0).start()
+    make_q(wq_ref, 0)
 
     def block(q_parts, state, start, slot, head, off, masked):
         k_blk = kv_buf[slot, head, 0, pl.ds(off, K_ROWS), :]
@@ -157,53 +187,106 @@
             acc_sc[state, a] = acc_sc[state, a] * alpha + jnp.dot(p_all, v_blk, preferred_element_type=jnp.float32)
 
     def load_q(head, qb):
-        sl = pl.ds(pl.multiple_of(qb * Q_ROWS, Q_ROWS), Q_ROWS)
-        return [jnp.concatenate([q_ref[head, sl, (a * per_chain + h) * head_dim:(a * per_chain + h + 1) * head_dim] for h in range(per_chain)], axis=0) for a in range(chains)]
-
-    per_pass = 2 * q_blocks
+        sl = row_slice(qb)
+        return [jnp.concatenate([q_sc[head, sl, (a * per_chain + h) * head_dim:(a * per_chain + h + 1) * head_dim] for h in range(per_chain)], axis=0) for a in range(chains)]
+
     per_piece = chunk_len // K_ROWS
 
     def step(s, carry):
-        phase = s // per_pass
-        head = lax.rem(s, per_pass) // q_blocks
+        phase = s // q_blocks
         qb = lax.rem(s, q_blocks)
-        state = lax.rem(s, per_pass)
-
-        def at(k, fn):
-            pl.when(s == k)(fn)
-
-        @pl.when(s == 5)
-        def _():
-            kv_copy(0).wait_recv()
-            kv_copy(2).start()
+        is_last = phase // 4
+        is_mid = (1 - is_last) * lax.rem(phase, 2)
+        is_first = 1 - is_last - is_mid
+        head = (1 - is_last) * (phase // 2) + is_last * (phase - 4)
+        state = head * q_blocks + qb
+
+        @pl.when(s == 0)
+        def _():
+            kv_copy(1, 0).wait_recv()
+
+        @pl.when(s == 1)
+        def _():
+            weight_copy(0, 1).wait_recv()
+            weight_copy(0, 3).start()
+
+        @pl.when(s == 2)
+        def _():
+            weight_copy(0, 2).wait_recv()
+            weight_copy(0, 3).wait_recv()
+            make_kv(wkv_sc, 1)
+            weight_copy(1, 0).wait_recv()
+            weight_copy(1, 1).start()
+            weight_copy(1, 2).start()
+
+        @pl.when(s == 3)
+        def _():
+            kv_copy(1, 1).start()
+            kv_copy(0, 1).start()
+            kv_copy(3, 1).start()
+            weight_copy(2, 0).start()
+            net.start(0, 0)
+            net.start(0, 1)
+            kv_copy(0, 0).wait_recv()
+            kv_copy(2, 0).start()
+
+        @pl.when(s == 4)
+        def _():
+            kv_copy(2, 0).wait_recv()
+
+        @pl.when(s == 6)
+        def _():
+            weight_copy(1, 1).wait_recv()
+            weight_copy(1, 3).start()
+            kv_copy(3, 0).wait_recv()
+            kv_copy(4, 0).start()
+            kv_copy(5, 0).start()
 
         @pl.when(s == 7)
         def _():
-            kv_copy(3).wait_recv()
-            kv_copy(4).start()
-            kv_copy(5).start()
+            weight_copy(1, 2).wait_recv()
+            weight_copy(1, 3).wait_recv()
+            make_q(wq_sc, 1)
 
         @pl.when(s == 8)
         def _():
-            kv_copy(2).wait_recv()
-
-        @pl.when(s == 11)
-        def _():
-            wo_copy(0).wait_recv()
-            wo_copy(1).start()
-            wo_copy(2).start()
+            kv_copy(1, 1).wait_recv()
+
+        @pl.when(s == 9)
+        def _():
+            kv_copy(0, 1).wait_recv()
+            kv_copy(2, 1).start()
+
+        @pl.when(s == 10)
+        def _():
+            kv_copy(3, 1).wait_recv()
+            kv_copy(4, 1).start()
+            kv_copy(5, 1).start()
+
+        @pl.when(s == 12)
+        def _():
+            kv_copy(2, 1).wait_recv()
+            weight_copy(2, 0).wait_recv()
+            weight_copy(2, 1).start()
+            weight_copy(2, 2).start()
+
+        @pl.when(s == 13)
+        def _():
+            kv_copy(4, 0).wait_recv()
+            kv_copy(6, 0).start()
 
         @pl.when(s == 14)
         def _():
-            kv_copy(4).wait_recv()
-            kv_copy(6).start()
+            kv_copy(4, 1).wait_recv()
+            kv_copy(6, 1).start()
 
         @pl.when(s == 16)
         def _():
-            kv_copy(5).wait_recv()
-            kv_copy(6).wait_recv()
-            wo_copy(1).wait_recv()
-            wo_copy(3).start()
+            for hd in range(2):
+                kv_copy(5, hd).wait_recv()
+                kv_copy(6, hd).wait_recv()
+            weight_copy(2, 1).wait_recv()
+            weight_copy(2, 3).start()
 
         for j, when in EARLY_FORWARD:
             @pl.when(s == when)
@@ -223,9 +306,6 @@
         q_parts = load_q(head, qb)
         start = qb * Q_ROWS
         diag = start // K_ROWS
-        is_first = (phase == 0).astype(jnp.int32)
-        is_last = (phase == 2).astype(jnp.int32)
-        is_mid = 1 - is_first - is_last
         count = is_first * (diag + per_piece * core_lower) + is_mid * 2 * per_piece * chip_lower + is_last * 4 * per_piece * y
         kv_head = head + is_last * (1 - 2 * head)
 
@@ -239,17 +319,17 @@
 
         lax.fori_loop(0, count, inner, 0)
 
-        @pl.when(phase == 0)
+        @pl.when(is_first == 1)
         def _():
             block(q_parts, state, start, 0, head, pl.multiple_of(diag * K_ROWS, K_ROWS), True)
 
         return carry
 
-    lax.fori_loop(0, 3 * per_pass, step, 0)
+    lax.fori_loop(0, 6 * q_blocks, step, 0)
 
     def finish(state, carry):
         head = state // q_blocks
-        sl = pl.ds(pl.multiple_of(lax.rem(state, q_blocks) * Q_ROWS, Q_ROWS), Q_ROWS)
+        sl = row_slice(lax.rem(state, q_blocks))
         for a in range(chains):
             total = jnp.sum(l_sc[state, a], axis=1, keepdims=True)
             out = (acc_sc[state, a] / total).astype(jnp.bfloat16)
@@ -257,7 +337,7 @@
                 o_ref[head, sl, (a * per_chain + h) * head_dim:(a * per_chain + h + 1) * head_dim] = out[h * Q_ROWS:(h + 1) * Q_ROWS]
         return carry
 
-    lax.fori_loop(0, per_pass, finish, 0)
+    lax.fori_loop(0, 2 * q_blocks, finish, 0)
 
     for e in range(2):
         late = c // 2
@@ -267,12 +347,14 @@
         kc_ref[e * chunk_len:(e + 1) * chunk_len] = kv_buf[slot, cross, 0]
         vc_ref[e * chunk_len:(e + 1) * chunk_len] = kv_buf[slot, cross, 1]
 
-    wo_copy(2).wait_recv()
-    wo_copy(3).wait_recv()
-    for n in range(7):
-        kv_copy(n).wait_send()
-    for n in range(4):
-        wo_copy(n).wait_send()
+    weight_copy(2, 2).wait_recv()
+    weight_copy(2, 3).wait_recv()
+    for hd in range(2):
+        for n in range(7):
+            kv_copy(n, hd).wait_send()
+    for kind in range(3):
+        for stage in range(4):
+            weight_copy(kind, stage).wait_send()
     forwarded = [j for j, _ in EARLY_FORWARD]
     second = [j for j, _ in EARLY_SECOND]
     for j in range(N_EARLY):
@@ -290,9 +372,9 @@
         net.sent(3, j)
 
 
-def attention(q, kv, wo, w1, w3, w2):
-    _, rows, width = q.shape
-    dim = w1.shape[0]
+def attention(x, gain, cos2, sin2, wq, wkv, wo, w1, w3, w2):
+    rows, dim = x.shape
+    width = wq.shape[1]
     states = 2 * rows // Q_ROWS
     m_rows = width // 128 // 2 * Q_ROWS
     vm = pl.BlockSpec(memory_space=pltpu.VMEM)
@@ -301,46 +383,50 @@
     n = N_EARLY
     return pl.pallas_call(
         attention_kernel,
-        in_specs=[vm, vm, hbm, hbm, hbm, hbm],
+        in_specs=[vm] * 6 + [hbm] * 4,
         out_specs=[vm, vm, vm, hbm, hbm, hbm, hbm],
         out_shape=[
-            jax.ShapeDtypeStruct(q.shape, bf16),
+            jax.ShapeDtypeStruct((2, rows, width), bf16),
             jax.ShapeDtypeStruct((2 * rows, 128), bf16),
             jax.ShapeDtypeStruct((2 * rows, 128), bf16),
-            jax.ShapeDtypeStruct((4, wo.shape[0] // 4, dim), bf16),
+            jax.ShapeDtypeStruct(wo.shape, bf16),
             jax.ShapeDtypeStruct((N_CHUNKS, 4, dim, TILE), bf16),
             jax.ShapeDtypeStruct((N_CHUNKS, 4, dim, TILE), bf16),
             jax.ShapeDtypeStruct((N_CHUNKS, 4, TILE, dim), bf16),
         ],
         scratch_shapes=[
-            pltpu.VMEM((8,) + kv.shape, bf16),
+            pltpu.VMEM((rows, dim), bf16),
+            pltpu.VMEM((2, rows, width), bf16),
+            pltpu.VMEM(wq.shape, bf16),
+            pltpu.VMEM(wkv.shape, bf16),
+            pltpu.VMEM((8, 2, 2, rows, 128), bf16),
             pltpu.VMEM((states, 2, m_rows, 128), jnp.float32),
             pltpu.VMEM((states, 2, m_rows, 128), jnp.float32),
             pltpu.VMEM((states, 2, m_rows, 128), jnp.float32),
             pltpu.SemaphoreType.DMA((n, 4, 3)),
             pltpu.SemaphoreType.DMA((n, 4, 3)),
-            pltpu.SemaphoreType.DMA((7,)),
-            pltpu.SemaphoreType.DMA((7,)),
-            pltpu.SemaphoreType.DMA((4,)),
-            pltpu.SemaphoreType.DMA((4,)),
+            pltpu.SemaphoreType.DMA((7, 2)),
+            pltpu.SemaphoreType.DMA((7, 2)),
+            pltpu.SemaphoreType.DMA((3, 4)),
+            pltpu.SemaphoreType.DMA((3, 4)),
         ],
         compiler_params=pltpu.CompilerParams(collective_id=0, has_side_effects=True, vmem_limit_bytes=VMEM_LIMIT),
         cost_estimate=pl.CostEstimate(flops=16 * rows * 4096 * width, bytes_accessed=32 * 2**20, transcendentals=rows * 4096 * 12),
         name="attention",
-    )(q, kv, wo, w1, w3, w2)
+    )(x, gain, cos2, sin2, wq, wkv, wo, w1, w3, w2)
 
 
 M_BLOCK = 512
-LATE_FORWARD = {0: (3,), 4: (4,), 9: (5,)}
-LATE_SECOND = {0: (2,), 5: (3,), 10: (4,)}
-END_FORWARD = {12: (6,), 14: (7,), 15: (8,)}
-END_SECOND = {12: (5,), 14: (6,), 15: (7,), 16: (8,)}
+LATE_FORWARD = {0: (4,), 4: (5,), 8: (6,)}
+LATE_SECOND = {0: (3,), 4: (4,), 8: (5,)}
+END_FORWARD = {12: (7,), 15: (8,)}
+END_SECOND = {12: (6,), 15: (7,), 16: (8,)}
 LOAD_AFTER = 12
 
 
-def mlp_kernel(b_ref, res_ref, w1_ref, w3_ref, w2_ref, a1_ref, a3_ref, a2_ref, out_ref, r1_ref, r3_ref, r2_ref,
-               w1_sc, w3_sc, w2_sc, acc_sc, load_sems, send_sems, recv_sems):
-    dim = b_ref.shape[1]
+def mlp_kernel(x_ref, gain_ref, o_ref, wo_ref, ro_ref, w1_ref, w3_ref, w2_ref, a1_ref, a3_ref, a2_ref, out_ref, r1_ref, r3_ref, r2_ref,
+               w1_sc, w3_sc, w2_sc, b_ref, acc_sc, load_sems, send_sems, recv_sems):
+    dim = x_ref.shape[1]
     width = 4 * TILE
     n_tiles = w1_ref.shape[1] // TILE
     net = Links((w1_ref, w3_ref, w2_ref), (r1_ref, r3_ref, r2_ref), send_sems, recv_sems, n_tiles)
@@ -378,11 +464,21 @@
         lax.fori_loop(0, b_ref.shape[0] // M_BLOCK, rows_step, 0)
 
     net.barrier()
-    net.start(0, 4)
-    net.start(0, 5)
+    net.start(0, N_EARLY)
+    net.start(0, N_EARLY + 1)
     for copy in own_loads(0, 0):
         copy.start()
-    acc_sc[...] = res_ref[...].astype(jnp.float32)
+
+    def residual_rows(i, carry):
+        sl = pl.ds(pl.multiple_of(i * Q_ROWS, Q_ROWS), Q_ROWS)
+        attn = jnp.dot(o_ref[0, sl, :], wo_ref[...], preferred_element_type=jnp.float32)
+        attn = attn + jnp.dot(o_ref[1, sl, :], ro_ref[...], preferred_element_type=jnp.float32)
+        residual = (x_ref[sl, :].astype(jnp.float32) + attn).astype(jnp.bfloat16).astype(jnp.float32)
+        acc_sc[sl, :] = residual
+        b_ref[sl, :] = normed_rows(residual, gain_ref[...].astype(jnp.float32))
+        return carry
+
+    lax.fori_loop(0, x_ref.shape[0] // Q_ROWS, residual_rows, 0)
     lane_tile = lax.broadcasted_iota(jnp.int32, (1, width), 1) // TILE
     source = 2 * lax.rem(lane_tile + net.c // 2, 2) + lax.rem(lane_tile // 2 + lax.rem(net.c, 2), 2)
 
@@ -395,22 +491,22 @@
                         net.arrived(0, j)
                     net.start(1, j)
                     net.start(2, j)
-                    if 6 <= j + 2 < N_CHUNKS:
+                    if N_EARLY + 2 <= j + 2 < N_CHUNKS:
                         net.start(0, j + 2)
         for when, chunks in second.items():
             @pl.when(s == when)
             def _(chunks=chunks):
                 for j in chunks:
-                    if j >= 3:
+                    if j >= 4:
                         net.arrived(1, j)
                     net.start(3, j)
 
     def load_next(s, slot, after):
-        for j in range(2, N_CHUNKS):
+        for j in range(3, N_CHUNKS):
             if (N_CHUNKS - 1 + j >= LOAD_AFTER) == after:
                 @pl.when(s == N_CHUNKS - 1 + j)
                 def _(j=j):
-                    if j >= 3:
+                    if j >= 4:
                         net.arrived(2, j)
                     net.arrived(3, j)
 
@@ -443,17 +539,17 @@
 
     lax.fori_loop(0, 2 * N_CHUNKS, step, 0)
     out_ref[...] = acc_sc[...].astype(out_ref.dtype)
+    for j in range(N_EARLY, N_CHUNKS):
+        net.sent(0, j)
     for j in range(4, N_CHUNKS):
-        net.sent(0, j)
-    for j in range(3, N_CHUNKS):
         net.sent(1, j)
         net.sent(2, j)
-    for j in range(2, N_CHUNKS):
+    for j in range(3, N_CHUNKS):
         net.sent(3, j)
 
 
-def mlp(b, res, w1, w3, w2, early):
-    rows, dim = b.shape
+def mlp(x, gain, o, wo, ro, w1, w3, w2, early):
+    rows, dim = x.shape
     vm = pl.BlockSpec(memory_space=pltpu.VMEM)
     hbm = pl.BlockSpec(memory_space=pl.ANY)
     bf16 = jnp.bfloat16
@@ -461,14 +557,15 @@
     n = N_CHUNKS
     return pl.pallas_call(
         mlp_kernel,
-        in_specs=[vm, vm] + [hbm] * 6,
+        in_specs=[vm] * 5 + [hbm] * 6,
         out_specs=[vm, hbm, hbm, hbm],
         out_shape=[jax.ShapeDtypeStruct((rows, dim), bf16)] + [jax.ShapeDtypeStruct(a.shape, bf16) for a in early],
-        input_output_aliases={5: 1, 6: 2, 7: 3},
+        input_output_aliases={8: 1, 9: 2, 10: 3},
         scratch_shapes=[
             pltpu.VMEM((2, dim, width), bf16),
             pltpu.VMEM((2, dim, width), bf16),
             pltpu.VMEM((2, width, dim), bf16),
+            pltpu.VMEM((rows, dim), bf16),
             pltpu.VMEM((rows, dim), jnp.float32),
             pltpu.SemaphoreType.DMA((2, 3)),
             pltpu.SemaphoreType.DMA((n, 4, 3)),
@@ -477,65 +574,24 @@
         compiler_params=pltpu.CompilerParams(collective_id=1, has_side_effects=True, vmem_limit_bytes=VMEM_LIMIT),
         cost_estimate=pl.CostEstimate(flops=12 * rows * dim * w1.shape[1], bytes_accessed=12 * dim * w1.shape[1], transcendentals=2 * rows * w1.shape[1]),
         name="mlp",
-    )(b, res, w1, w3, w2, *early)[0]
+    )(x, gain, o, wo, ro, w1, w3, w2, *early)[0]
 
 def solution(mesh):
-    cp_size = mesh.shape["cp"]
-    tp_swap = [(0, 1), (1, 0)]
-    chip_swap = [(0, 2), (2, 0), (1, 3), (3, 1)]
-    core_swap = [(0, 1), (1, 0), (2, 3), (3, 2)]
-
-    def swap_tp(a):
-        return lax.ppermute(a, "tp", tp_swap)
-
-    def swap_chip(a):
-        return lax.ppermute(a, "cp", chip_swap)
-
-    def swap_core(a):
-        return lax.ppermute(a, "cp", core_swap)
-
-    def spread(a):
-        b = swap_chip(a)
-        return [a, b, swap_core(a), swap_core(b)]
+    n_pieces = 2 * mesh.shape["cp"]
 
     def layer_shard(x_loc, norm_attn, norm_mlp, w_query, w_key, w_value, w_out, w_gate, w_up, w_down):
         tok_dev, dim = x_loc.shape
         local_q, head_dim = w_query.shape[1], w_query.shape[2]
         cp_index = lax.axis_index("cp")
-        tp_index = lax.axis_index("tp")
-        n_pieces = 2 * cp_size
-        piece = jnp.where(tp_index == 0, cp_index, n_pieces - 1 - cp_index)
-        tables = rope_tables(piece * tok_dev + jnp.arange(tok_dev, dtype=jnp.int32), head_dim)
-
-        peers = jnp.arange(cp_size, dtype=jnp.int32) ^ cp_index
-        rel_slot = jnp.where(peers == 1, 2, jnp.where(peers == 2, 1, peers))
-
+        piece = jnp.where(lax.axis_index("tp") == 0, cp_index, n_pieces - 1 - cp_index)
+        cosine, sine_tab = rope_tables(piece * tok_dev + jnp.arange(tok_dev, dtype=jnp.int32), head_dim)
+        cos2 = jnp.concatenate([cosine, cosine], axis=1)
+        sin2 = jnp.concatenate([-sine_tab, sine_tab], axis=1)
         wq = w_query.reshape(dim, local_q * head_dim)
         wkv = jnp.concatenate([w_key.reshape(dim, -1), w_value.reshape(dim, -1)], axis=1)
         wo = w_out.reshape(local_q * head_dim, dim)
-
-        def other_half_rows(w):
-            quarter = w.shape[0] // cp_size
-            own = lax.dynamic_slice_in_dim(w, cp_index * quarter, quarter, axis=0)
-            stack = jnp.stack(spread(swap_tp(own)))
-            return jnp.take(stack, rel_slot, axis=0).reshape(w.shape)
-
-        wkv_other = other_half_rows(wkv)
-        wq_other = other_half_rows(wq)
-
-        normed = rms_norm(x_loc, norm_attn)
-        dot = functools.partial(jnp.dot, preferred_element_type=jnp.float32)
-
-        def kv_pair(w):
-            proj = dot(normed, w)
-            return jnp.stack([rope_rotate(proj[:, :head_dim], tables, head_dim), proj[:, head_dim:].astype(jnp.bfloat16)])
-
-        kv = jnp.stack([kv_pair(wkv), kv_pair(wkv_other)])
-        q = jnp.stack([rope_rotate(dot(normed, wq), tables, head_dim), rope_rotate(dot(normed, wq_other), tables, head_dim)])
-        o, k_cache, v_cache, wo_parts, *early = attention(q, kv, wo, w_gate, w_up, w_down)
-        wo_other = jnp.take(wo_parts, rel_slot, axis=0).reshape(wo.shape)
-        residual = (x_loc.astype(jnp.float32) + (dot(o[0], wo) + dot(o[1], wo_other))).astype(jnp.bfloat16)
-        layer_out = mlp(rms_norm(residual, norm_mlp), residual, w_gate, w_up, w_down, early)
+        o, k_cache, v_cache, wo_other, *early = attention(x_loc, norm_attn[None], cos2, sin2, wq, wkv, wo, w_gate, w_up, w_down)
+        layer_out = mlp(x_loc, norm_mlp[None], o, wo, wo_other, w_gate, w_up, w_down, early)
         return layer_out, k_cache, v_cache
 
     row_spec = P(("dp", "cp", "tp"), None)

time: 463 us -> 376 us (0.81)
  other arithmetic: 30.3 us -> 5.31 us
  local copies, waits for them, and re-layouts: 33.3 us -> 13.3 us
  matrix products: 17.4 us -> 0 us
  waiting for transfers between devices: 10.4 us -> 0 us
  starting transfers between devices: 8.68 us -> 0 us
    dot_general x6 -> x0, matrix products: 17.4 us -> none  [the longest x1 4.31 us: layer_shard(): dot(normed, wq)]
    concatenate x4 -> x1, other arithmetic: 14.3 us -> 1.31 us  [layer_shard(): cos2 = jnp.concatenate([cosine, cosine], axis=1)]
    ppermute x8 -> x0, waiting for transfers between devices: 10.4 us -> none  [the longest x2 9.91 us: swap_chip(): return lax.ppermute(a, 'cp', chip_swap)]
    gather x4 -> x0, local copies, waits for them, and re-layouts: 10.1 us -> none  [the longest x3 7.74 us: other_half_rows(): return jnp.take(stack, rel_slot, axis=0).reshape(w.shape)]
    concatenate x2 -> x0, local copies, waits for them, and re-layouts: 8.87 us -> none  [rope_rotate(): return jnp.concatenate(parts, axis=1).astype(jnp.bfloat16)]
    ppermute x8 -> x0, starting transfers between devices: 8.68 us -> none  [the longest x4 4.59 us: swap_core(): return lax.ppermute(a, 'cp', core_swap)]
    another operation x5 -> x0, other arithmetic: 6.83 us -> none  [the longest x2 3.51 us: other_half_rows(): stack = jnp.stack(spread(swap_tp(own)))]
    unnamed x42 -> x8, local copies, waits for them, and re-layouts: 11.5 us -> 8.27 us
  transfers between devices with their start and end apart: 8 -> 0, of which waited for: 3 -> 0; matrix products, arithmetic and copies ran while one was open for 7% -> 0% of each run, Pallas kernels for 0% -> 0%
where the time goes in v1:
time: 376 us; the launch traced here: 373 us
  Pallas kernels  354 us (94%)
  local copies, waits for them, and re-layouts  13.3 us (4%)
  other arithmetic  5.31 us (1%)
    pallas_call x1, Pallas kernels, attention(): pl.pallas_call(attention_kernel, in_specs=[vm] * 6 + [hbm] * 4, out_specs...  196 us
    pallas_call x1, Pallas kernels, mlp(): pl.pallas_call(mlp_kernel, in_specs=[vm] * 5 + [hbm] * 6, out_specs=[vm,...  158 us
    unnamed x8, local copies, waits for them, and re-layouts  8.27 us

profile of v1, /device:TPU:5, one launch (start us, length us, event | category | flops | bytes accessed | tf_op | source)
XLA Modules:
  0.0 372.9 jit_solution(5067768219189364012)
XLA Ops:
  0.7 1.3 broadcast_in_dim.9.gain_ref
  2.0 1.3 broadcast_in_dim.8.gain_ref
  3.2 2.1 pad_maximum_fusion.wkv_ref
  5.3 1.9 fusion
  7.2 1.3 pad_maximum_fusion.1
  8.5 2.8 copy.17
  11.4 2.4 copy.18.wq_ref
  13.8 195.8 %attention.1 = (bf16[2,1024,768]{2,1,0:T(8,128)(2,1)}, bf16[2048,128]{1,0:T(8,128)(2,1)}, bf16[2048,128]{1,0:T(8,128)(2,1)}, bf16[768,1536]{1,0:T(8,128)(2,1)}, ...) custom-call(bf16[1024,1536]{1,0:T(8,128)(2,1)} %x_ref.3, ...), custom_call_target="tpu_custom_call" | custom-call | flops 51539607552 | bytes 33554432 | tf_op jit(solution)/shard_map/attention/pallas_call | solution.py:384
  209.6 157.9 %mlp.1 = (bf16[1024,1536]{1,0:T(8,128)(2,1)}, bf16[9,4,1536,128]{3,2,1,0:T(8,128)(2,1)}, bf16[9,4,1536,128]{3,2,1,0:T(8,128)(2,1)}, bf16[9,4,128,1536]{3,2,1,0:T(8,128)(2,1)}) custom-call(bf16[1024,1536]{1,0:T(8,128)(2,1)} %x_ref.3, bf16[1,1536]{1,0:T(2,128)(2,1)} %broadcast_in_dim.8.gain_ref, ...), custom_call_target="tpu_custom_call", output_to_operand_aliasing={{1}: (8, {}), {2}: (9, {}), {3}: (10, {})} | custom-call | flops 84557168640 | bytes 82575360 | tf_op jit(solution)/shard_map/mlp/pallas_call | solution.py:558
  367.5 0.0 copy-start.1
  367.5 0.0 copy-start
  367.5 3.8 %copy.25 = bf16[1024,1536]{1,0:T(8,128)(2,1)} copy(bf16[1024,1536]{1,0:T(8,128)(2,1)} %get-tuple-element.27) | data formatting | bytes 6291456
  371.4 0.0 copy-done.1
  371.4 0.8 copy.26
  372.1 0.0 copy-done
  372.2 0.8 copy.27
  (2 shorter events, 0.0 us)
Async XLA Ops:
  367.5 3.9 %copy-start.1 = (bf16[2048,128]{1,0:T(8,128)(2,1)S(1)}, bf16[2048,128]{1,0:T(8,128)(2,1)}, u32[]{:S(2)}) copy-start(bf16[2048,128]{1,0:T(8,128)(2,1)} %get-tuple-element.28) | copy-start | bytes 1572868
  367.5 4.7 %copy-start = (bf16[2048,128]{1,0:T(8,128)(2,1)S(1)}, bf16[2048,128]{1,0:T(8,128)(2,1)}, u32[]{:S(2)}) copy-start(bf16[2048,128]{1,0:T(8,128)(2,1)} %get-tuple-element.29) | copy-start | bytes 1572868

commit v2 on v1

--- a/solution.py
+++ b/solution.py
@@ -17,7 +17,7 @@
 MESH = pl.DeviceIdType.MESH
 TILE = 128
 N_CHUNKS = 9
-N_EARLY = 5
+N_EARLY = 9
 
 
 def rope_tables(positions, head_dim):
@@ -355,21 +355,21 @@
     for kind in range(3):
         for stage in range(4):
             weight_copy(kind, stage).wait_send()
-    forwarded = [j for j, _ in EARLY_FORWARD]
-    second = [j for j, _ in EARLY_SECOND]
-    for j in range(N_EARLY):
-        if j not in forwarded:
-            net.arrived(0, j)
-        net.sent(0, j)
-    for j in forwarded:
-        if j not in second:
-            net.arrived(1, j)
+    for j in range(4, N_CHUNKS):
+        net.arrived(0, j)
+        net.start(1, j)
+        net.start(2, j)
+        if j + 2 < N_CHUNKS:
+            net.start(0, j + 2)
+        net.arrived(1, j - 1)
+        net.start(3, j - 1)
+    net.arrived(1, N_CHUNKS - 1)
+    net.start(3, N_CHUNKS - 1)
+    for j in range(N_CHUNKS):
         net.arrived(2, j)
-        net.sent(1, j)
-        net.sent(2, j)
-    for j in second:
         net.arrived(3, j)
-        net.sent(3, j)
+        for stage in range(4):
+            net.sent(stage, j)
 
 
 def attention(x, gain, cos2, sin2, wq, wkv, wo, w1, w3, w2):
@@ -417,10 +417,10 @@
 
 
 M_BLOCK = 512
-LATE_FORWARD = {0: (4,), 4: (5,), 8: (6,)}
-LATE_SECOND = {0: (3,), 4: (4,), 8: (5,)}
-END_FORWARD = {12: (7,), 15: (8,)}
-END_SECOND = {12: (6,), 15: (7,), 16: (8,)}
+LATE_FORWARD = {}
+LATE_SECOND = {}
+END_FORWARD = {}
+END_SECOND = {}
 LOAD_AFTER = 12
 
 
@@ -463,9 +463,6 @@
 
         lax.fori_loop(0, b_ref.shape[0] // M_BLOCK, rows_step, 0)
 
-    net.barrier()
-    net.start(0, N_EARLY)
-    net.start(0, N_EARLY + 1)
     for copy in own_loads(0, 0):
         copy.start()
 
@@ -502,7 +499,7 @@
                     net.start(3, j)
 
     def load_next(s, slot, after):
-        for j in range(3, N_CHUNKS):
+        for j in range(N_EARLY, N_CHUNKS):
             if (N_CHUNKS - 1 + j >= LOAD_AFTER) == after:
                 @pl.when(s == N_CHUNKS - 1 + j)
                 def _(j=j):
@@ -539,13 +536,6 @@
 
     lax.fori_loop(0, 2 * N_CHUNKS, step, 0)
     out_ref[...] = acc_sc[...].astype(out_ref.dtype)
-    for j in range(N_EARLY, N_CHUNKS):
-        net.sent(0, j)
-    for j in range(4, N_CHUNKS):
-        net.sent(1, j)
-        net.sent(2, j)
-    for j in range(3, N_CHUNKS):
-        net.sent(3, j)
 
 
 def mlp(x, gain, o, wo, ro, w1, w3, w2, early):
@@ -571,7 +561,7 @@
             pltpu.SemaphoreType.DMA((n, 4, 3)),
             pltpu.SemaphoreType.DMA((n, 4, 3)),
         ],
-        compiler_params=pltpu.CompilerParams(collective_id=1, has_side_effects=True, vmem_limit_bytes=VMEM_LIMIT),
+        compiler_params=pltpu.CompilerParams(vmem_limit_bytes=VMEM_LIMIT),
         cost_estimate=pl.CostEstimate(flops=12 * rows * dim * w1.shape[1], bytes_accessed=12 * dim * w1.shape[1], transcendentals=2 * rows * w1.shape[1]),
         name="mlp",
     )(x, gain, o, wo, ro, w1, w3, w2, *early)[0]

time: 376 us -> 465 us (1.24)
  Pallas kernels: 354 us -> 449 us
    pallas_call x1, Pallas kernels: 196 us -> 328 us  [attention(): pl.pallas_call(attention_kernel, in_specs=[vm] * 6 + [hbm] * 4, out_specs...]
    pallas_call x1, Pallas kernels: 158 us -> 121 us  [mlp(): pl.pallas_call(mlp_kernel, in_specs=[vm] * 5 + [hbm] * 6, out_specs=[vm,...]
where the time goes in v2:
time: 465 us
  Pallas kernels  449 us (97%)
  local copies, waits for them, and re-layouts  9.44 us (2%)
  other arithmetic  5.3 us (1%)
    pallas_call x1, Pallas kernels, attention(): pl.pallas_call(attention_kernel, in_specs=[vm] * 6 + [hbm] * 4, out_specs...  328 us
    pallas_call x1, Pallas kernels, mlp(): pl.pallas_call(mlp_kernel, in_specs=[vm] * 5 + [hbm] * 6, out_specs=[vm,...  121 us

profile of v2, /device:TPU:5, one launch (start us, length us, event | category | flops | bytes accessed | tf_op | source)
XLA Modules:
  0.0 464.6 jit_solution(8965967341880877992)
XLA Ops:
  0.7 1.3 broadcast_in_dim.9.gain_ref
  2.0 1.3 broadcast_in_dim.8.gain_ref
  3.2 2.1 pad_maximum_fusion.wkv_ref
  5.3 1.9 fusion
  7.2 1.3 pad_maximum_fusion.1
  8.5 2.8 copy.17
  11.4 2.4 copy.18.wq_ref
  13.8 328.2 %attention.1 = (bf16[2,1024,768]{2,1,0:T(8,128)(2,1)}, bf16[2048,128]{1,0:T(8,128)(2,1)}, bf16[2048,128]{1,0:T(8,128)(2,1)}, bf16[768,1536]{1,0:T(8,128)(2,1)}, ...) custom-call(bf16[1024,1536]{1,0:T(8,128)(2,1)} %x_ref.3, ...), custom_call_target="tpu_custom_call" | custom-call | flops 51539607552 | bytes 33554432 | tf_op jit(solution)/shard_map/attention/pallas_call | solution.py:384
  342.0 0.0 copy-start.1
  342.0 0.0 copy-start
  342.0 121.0 %mlp.1 = (bf16[1024,1536]{1,0:T(8,128)(2,1)}, bf16[9,4,1536,128]{3,2,1,0:T(8,128)(2,1)}, bf16[9,4,1536,128]{3,2,1,0:T(8,128)(2,1)}, bf16[9,4,128,1536]{3,2,1,0:T(8,128)(2,1)}) custom-call(bf16[1024,1536]{1,0:T(8,128)(2,1)} %x_ref.3, bf16[1,1536]{1,0:T(2,128)(2,1)} %broadcast_in_dim.8.gain_ref, ...), custom_call_target="tpu_custom_call", output_to_operand_aliasing={{1}: (8, {}), {2}: (9, {}), {3}: (10, {})} | custom-call | flops 84557168640 | bytes 82575360 | tf_op jit(solution)/shard_map/mlp/pallas_call | solution.py:548
  463.0 0.0 copy-done.1
  463.0 0.8 copy.24
  463.8 0.0 copy-done
  463.8 0.8 copy.25
  (2 shorter events, 0.0 us)
Async XLA Ops:
  342.0 121.0 %copy-start.1 = (bf16[2048,128]{1,0:T(8,128)(2,1)S(1)}, bf16[2048,128]{1,0:T(8,128)(2,1)}, u32[]{:S(2)}) copy-start(bf16[2048,128]{1,0:T(8,128)(2,1)} %get-tuple-element.28) | copy-start | bytes 1572868
  342.0 121.8 %copy-start = (bf16[2048,128]{1,0:T(8,128)(2,1)S(1)}, bf16[2048,128]{1,0:T(8,128)(2,1)}, u32[]{:S(2)}) copy-start(bf16[2048,128]{1,0:T(8,128)(2,1)} %get-tuple-element.29) | copy-start | bytes 1572868

commit v3 on v1

--- a/solution.py
+++ b/solution.py
@@ -22,9 +22,11 @@
 
 def rope_tables(positions, head_dim):
     half_dim = head_dim // 2
-    inv_freq = ROPE_BASE ** (-2.0 * jnp.arange(half_dim, dtype=jnp.float32) / head_dim)
+    lane = jnp.arange(head_dim, dtype=jnp.int32)
+    inv_freq = ROPE_BASE ** (-2.0 * (lane % half_dim).astype(jnp.float32) / head_dim)
     angles = positions.astype(jnp.float32)[:, None] * inv_freq[None, :]
-    return jnp.cos(angles), jnp.sin(angles)
+    sine_tab = jnp.sin(angles)
+    return jnp.cos(angles), jnp.where(lane < half_dim, -sine_tab, sine_tab)
 
 
 class Links:
@@ -53,7 +55,7 @@
         copies = []
         for a in range(3):
             if stage == 0:
-                tile = jnp.minimum(4 * j + self.c, self.n_tiles - 1)
+                tile = 4 * j + self.c
                 sl = pl.ds(pl.multiple_of(tile * TILE, TILE), TILE)
                 src = self.weights[a].at[sl, :] if a == 2 else self.weights[a].at[:, sl]
             else:
@@ -61,6 +63,35 @@
             copies.append(self.remote(src, self.recv[a].at[j, stage], self.send_sems.at[j, stage, a], self.recv_sems.at[j, stage, a], to))
         return copies
 
+    def last_chunk(self, stage, last):
+        half = lax.rem(self.c, 2)
+        begin = (self.n_tiles // 4) * 4 * TILE
+        copies = []
+        for a in range(3):
+            depth = last[a].shape[0] // 2
+            at = pl.ds(pl.multiple_of(half * depth, 64), depth)
+            dst = last[a].at[at, :]
+            if stage == 2:
+                src = dst
+            elif a == 2:
+                src = self.weights[a].at[pl.ds(pl.multiple_of(begin + half * depth, 64), depth), :]
+            else:
+                src = self.weights[a].at[at, pl.ds(begin, last[a].shape[1])]
+            j = N_CHUNKS - 1
+            copies.append(self.remote(src, dst, self.send_sems.at[j, stage, a], self.recv_sems.at[j, stage, a], "y.d"[stage]))
+        return copies
+
+    def pass_on(self, j):
+        for first, over_x, over_d in zip(self.chunk(0, j), self.chunk(1, j), self.chunk(2, j)):
+            first.wait_recv()
+            over_x.start()
+            over_d.start()
+
+    def pass_second(self, j):
+        for first, over_d in zip(self.chunk(1, j), self.chunk(3, j)):
+            first.wait_recv()
+            over_d.start()
+
     def start(self, stage, j):
         for copy in self.chunk(stage, j):
             copy.start()
@@ -84,14 +115,13 @@
     return (wide * inv_rms * gain).astype(jnp.bfloat16)
 
 
-def attention_kernel(x_ref, gain_ref, cos_ref, sin_ref, wq_ref, wkv_ref, wo_ref, w1_ref, w3_ref, w2_ref,
+def attention_kernel(x_ref, gain_ref, cos_ref, sin_ref, wq_ref, wk_ref, wv_ref, wo_ref, w1_ref, w3_ref, w2_ref,
                      o_ref, kc_ref, vc_ref, ro_ref, r1_ref, r3_ref, r2_ref,
-                     a_sc, q_sc, wq_sc, wkv_sc, kv_buf, m_sc, l_sc, acc_sc, send_sems, recv_sems, kv_send, kv_recv, wt_send, wt_recv):
+                     a_sc, q_sc, wq_sc, wk_sc, wv_sc, kv_buf, m_sc, l_sc, acc_sc, send_sems, recv_sems, kv_send, kv_recv, wt_send, wt_recv):
     head_dim = 128
     half_dim = head_dim // 2
     chunk_len = x_ref.shape[0]
-    width = wq_ref.shape[1]
-    heads = width // head_dim
+    heads = wq_ref.shape[0]
     chains = 2
     per_chain = heads // chains
     rows = per_chain * Q_ROWS
@@ -108,11 +138,20 @@
         return net.remote(kv_buf.at[src, hd], kv_buf.at[dst, hd], kv_send.at[n, hd], kv_recv.at[n, hd], to)
 
     def weight_copy(kind, stage):
-        own, held = ((wkv_ref, wkv_sc), (wq_ref, wq_sc), (wo_ref, ro_ref))[kind]
-        quarter = own.shape[0] // 4
+        own, held = ((wk_ref, wk_sc), (wv_ref, wv_sc), (wq_ref, wq_sc), (wo_ref, ro_ref))[kind]
+        quarter = own.shape[-2] // 4
         sl = pl.ds(pl.multiple_of((other_chip if stage == 3 else c) * quarter, 64), quarter)
         src = own if stage == 0 else held
-        return net.remote(src.at[sl, :], held.at[sl, :], wt_send.at[kind, stage], wt_recv.at[kind, stage], "yxdd"[stage])
+        pick = (lambda r: r.at[sl, :]) if kind == 3 else (lambda r: r.at[:, sl, :])
+        return net.remote(pick(src), pick(held), wt_send.at[kind, stage], wt_recv.at[kind, stage], "yxdd"[stage])
+
+    def weights_start(kinds, stage):
+        for kind in kinds:
+            weight_copy(kind, stage).start()
+
+    def weights_arrived(kinds, stage):
+        for kind in kinds:
+            weight_copy(kind, stage).wait_recv()
 
     def row_slice(i):
         return pl.ds(pl.multiple_of(i * Q_ROWS, Q_ROWS), Q_ROWS)
@@ -123,14 +162,15 @@
     def norm_x():
         def body(i, carry):
             sl = row_slice(i)
-            a_sc[sl, :] = normed_rows(x_ref[sl, :].astype(jnp.float32), gain_ref[...].astype(jnp.float32))
+            a_sc[sl, :] = normed_rows(x_ref[sl, :].astype(jnp.float32), gain_ref[...].astype(jnp.float32)[None, :])
             return carry
         lax.fori_loop(0, q_blocks, body, 0)
 
-    def make_kv(w_ref, hd):
+    def make_kv(k_ref, v_ref, hd):
         def body(i, carry):
             sl = row_slice(i)
-            proj = jnp.dot(a_sc[sl, :], w_ref[...], preferred_element_type=jnp.float32)
+            w = jnp.concatenate([k_ref[0], v_ref[0]], axis=1)
+            proj = jnp.dot(a_sc[sl, :], w, preferred_element_type=jnp.float32)
             kv_buf[0, hd, 0, sl, :] = rope(proj[:, :head_dim], sl)
             kv_buf[0, hd, 1, sl, :] = proj[:, head_dim:].astype(jnp.bfloat16)
             return carry
@@ -139,7 +179,8 @@
     def make_q(w_ref, hd):
         def body(i, carry):
             sl = row_slice(i)
-            proj = jnp.dot(a_sc[sl, :], w_ref[...], preferred_element_type=jnp.float32)
+            w = jnp.concatenate([w_ref[h] for h in range(heads)], axis=1)
+            proj = jnp.dot(a_sc[sl, :], w, preferred_element_type=jnp.float32)
             for h in range(heads):
                 cols = slice(h * head_dim, (h + 1) * head_dim)
                 q_sc[hd, sl, cols] = rope(proj[:, cols], sl)
@@ -147,16 +188,15 @@
         lax.fori_loop(0, q_blocks, body, 0)
 
     net.barrier()
-    weight_copy(0, 0).start()
-    weight_copy(1, 0).start()
+    weights_start((0, 1, 2), 0)
     norm_x()
-    make_kv(wkv_ref, 0)
+    make_kv(wk_ref, wv_ref, 0)
     m_sc[...] = jnp.full_like(m_sc, MASK_VALUE)
     l_sc[...] = jnp.zeros_like(l_sc)
     acc_sc[...] = jnp.zeros_like(acc_sc)
-    weight_copy(0, 0).wait_recv()
-    weight_copy(0, 1).start()
-    weight_copy(0, 2).start()
+    weights_arrived((0, 1), 0)
+    weights_start((0, 1), 1)
+    weights_start((0, 1), 2)
     kv_copy(1, 0).start()
     kv_copy(0, 0).start()
     kv_copy(3, 0).start()
@@ -207,24 +247,24 @@
 
         @pl.when(s == 1)
         def _():
-            weight_copy(0, 1).wait_recv()
-            weight_copy(0, 3).start()
+            weights_arrived((0, 1), 1)
+            weights_start((0, 1), 3)
 
         @pl.when(s == 2)
         def _():
-            weight_copy(0, 2).wait_recv()
-            weight_copy(0, 3).wait_recv()
-            make_kv(wkv_sc, 1)
-            weight_copy(1, 0).wait_recv()
-            weight_copy(1, 1).start()
-            weight_copy(1, 2).start()
+            weights_arrived((0, 1), 2)
+            weights_arrived((0, 1), 3)
+            make_kv(wk_sc, wv_sc, 1)
+            weights_arrived((2,), 0)
+            weights_start((2,), 1)
+            weights_start((2,), 2)
 
         @pl.when(s == 3)
         def _():
             kv_copy(1, 1).start()
             kv_copy(0, 1).start()
             kv_copy(3, 1).start()
-            weight_copy(2, 0).start()
+            weights_start((3,), 0)
             net.start(0, 0)
             net.start(0, 1)
             kv_copy(0, 0).wait_recv()
@@ -236,16 +276,16 @@
 
         @pl.when(s == 6)
         def _():
-            weight_copy(1, 1).wait_recv()
-            weight_copy(1, 3).start()
+            weights_arrived((2,), 1)
+            weights_start((2,), 3)
             kv_copy(3, 0).wait_recv()
             kv_copy(4, 0).start()
             kv_copy(5, 0).start()
 
         @pl.when(s == 7)
         def _():
-            weight_copy(1, 2).wait_recv()
-            weight_copy(1, 3).wait_recv()
+            weights_arrived((2,), 2)
+            weights_arrived((2,), 3)
             make_q(wq_sc, 1)
 
         @pl.when(s == 8)
@@ -266,9 +306,9 @@
         @pl.when(s == 12)
         def _():
             kv_copy(2, 1).wait_recv()
-            weight_copy(2, 0).wait_recv()
-            weight_copy(2, 1).start()
-            weight_copy(2, 2).start()
+            weights_arrived((3,), 0)
+            weights_start((3,), 1)
+            weights_start((3,), 2)
 
         @pl.when(s == 13)
         def _():
@@ -285,23 +325,20 @@
             for hd in range(2):
                 kv_copy(5, hd).wait_recv()
                 kv_copy(6, hd).wait_recv()
-            weight_copy(2, 1).wait_recv()
-            weight_copy(2, 3).start()
+            weights_arrived((3,), 1)
+            weights_start((3,), 3)
 
         for j, when in EARLY_FORWARD:
             @pl.when(s == when)
             def _(j=j):
-                net.arrived(0, j)
-                net.start(1, j)
-                net.start(2, j)
+                net.pass_on(j)
                 if j + 2 < N_EARLY:
                     net.start(0, j + 2)
 
         for j, when in EARLY_SECOND:
             @pl.when(s == when)
             def _(j=j):
-                net.arrived(1, j)
-                net.start(3, j)
+                net.pass_second(j)
 
         q_parts = load_q(head, qb)
         start = qb * Q_ROWS
@@ -347,12 +384,12 @@
         kc_ref[e * chunk_len:(e + 1) * chunk_len] = kv_buf[slot, cross, 0]
         vc_ref[e * chunk_len:(e + 1) * chunk_len] = kv_buf[slot, cross, 1]
 
-    weight_copy(2, 2).wait_recv()
-    weight_copy(2, 3).wait_recv()
+    weights_arrived((3,), 2)
+    weights_arrived((3,), 3)
     for hd in range(2):
         for n in range(7):
             kv_copy(n, hd).wait_send()
-    for kind in range(3):
+    for kind in range(4):
         for stage in range(4):
             weight_copy(kind, stage).wait_send()
     forwarded = [j for j, _ in EARLY_FORWARD]
@@ -372,9 +409,9 @@
         net.sent(3, j)
 
 
-def attention(x, gain, cos2, sin2, wq, wkv, wo, w1, w3, w2):
+def attention(x, gain, cos2, sin2, wq, wk, wv, wo, w1, w3, w2):
     rows, dim = x.shape
-    width = wq.shape[1]
+    width = wq.shape[0] * 128
     states = 2 * rows // Q_ROWS
     m_rows = width // 128 // 2 * Q_ROWS
     vm = pl.BlockSpec(memory_space=pltpu.VMEM)
@@ -383,22 +420,23 @@
     n = N_EARLY
     return pl.pallas_call(
         attention_kernel,
-        in_specs=[vm] * 6 + [hbm] * 4,
+        in_specs=[vm] * 7 + [hbm] * 4,
         out_specs=[vm, vm, vm, hbm, hbm, hbm, hbm],
         out_shape=[
             jax.ShapeDtypeStruct((2, rows, width), bf16),
             jax.ShapeDtypeStruct((2 * rows, 128), bf16),
             jax.ShapeDtypeStruct((2 * rows, 128), bf16),
             jax.ShapeDtypeStruct(wo.shape, bf16),
-            jax.ShapeDtypeStruct((N_CHUNKS, 4, dim, TILE), bf16),
-            jax.ShapeDtypeStruct((N_CHUNKS, 4, dim, TILE), bf16),
-            jax.ShapeDtypeStruct((N_CHUNKS, 4, TILE, dim), bf16),
+            jax.ShapeDtypeStruct((N_CHUNKS - 1, 4, dim, TILE), bf16),
+            jax.ShapeDtypeStruct((N_CHUNKS - 1, 4, dim, TILE), bf16),
+            jax.ShapeDtypeStruct((N_CHUNKS - 1, 4, TILE, dim), bf16),
         ],
         scratch_shapes=[
             pltpu.VMEM((rows, dim), bf16),
             pltpu.VMEM((2, rows, width), bf16),
             pltpu.VMEM(wq.shape, bf16),
-            pltpu.VMEM(wkv.shape, bf16),
+            pltpu.VMEM(wk.shape, bf16),
+            pltpu.VMEM(wv.shape, bf16),
             pltpu.VMEM((8, 2, 2, rows, 128), bf16),
             pltpu.VMEM((states, 2, m_rows, 128), jnp.float32),
             pltpu.VMEM((states, 2, m_rows, 128), jnp.float32),
@@ -407,30 +445,31 @@
             pltpu.SemaphoreType.DMA((n, 4, 3)),
             pltpu.SemaphoreType.DMA((7, 2)),
             pltpu.SemaphoreType.DMA((7, 2)),
-            pltpu.SemaphoreType.DMA((3, 4)),
-            pltpu.SemaphoreType.DMA((3, 4)),
+            pltpu.SemaphoreType.DMA((4, 4)),
+            pltpu.SemaphoreType.DMA((4, 4)),
         ],
         compiler_params=pltpu.CompilerParams(collective_id=0, has_side_effects=True, vmem_limit_bytes=VMEM_LIMIT),
         cost_estimate=pl.CostEstimate(flops=16 * rows * 4096 * width, bytes_accessed=32 * 2**20, transcendentals=rows * 4096 * 12),
         name="attention",
-    )(x, gain, cos2, sin2, wq, wkv, wo, w1, w3, w2)
+    )(x, gain, cos2, sin2, wq, wk, wv, wo, w1, w3, w2)
 
 
 M_BLOCK = 512
-LATE_FORWARD = {0: (4,), 4: (5,), 8: (6,)}
-LATE_SECOND = {0: (3,), 4: (4,), 8: (5,)}
-END_FORWARD = {12: (7,), 15: (8,)}
-END_SECOND = {12: (6,), 15: (7,), 16: (8,)}
+LATE_FORWARD = {3: (5,), 7: (6,)}
+LATE_SECOND = {3: (4,), 8: (5,)}
+END_FORWARD = {12: (7,)}
+END_SECOND = {12: (6,), 15: (7,)}
 LOAD_AFTER = 12
 
 
-def mlp_kernel(x_ref, gain_ref, o_ref, wo_ref, ro_ref, w1_ref, w3_ref, w2_ref, a1_ref, a3_ref, a2_ref, out_ref, r1_ref, r3_ref, r2_ref,
+def mlp_kernel(x_ref, gain_ref, o_ref, wo_ref, ro_ref, w1_ref, w3_ref, w2_ref, a1_ref, a3_ref, a2_ref, out_ref, r1_ref, r3_ref, r2_ref, e1_ref, e3_ref, e2_ref,
                w1_sc, w3_sc, w2_sc, b_ref, acc_sc, load_sems, send_sems, recv_sems):
     dim = x_ref.shape[1]
     width = 4 * TILE
     n_tiles = w1_ref.shape[1] // TILE
     net = Links((w1_ref, w3_ref, w2_ref), (r1_ref, r3_ref, r2_ref), send_sems, recv_sems, n_tiles)
     own_last = (n_tiles - 4) * TILE
+    ends = (e1_ref, e3_ref, e2_ref)
 
     def own_loads(j, slot):
         off = min(j * width, own_last) if isinstance(j, int) else pl.multiple_of(jnp.minimum(j * width, own_last), TILE)
@@ -449,6 +488,14 @@
             copies.append(pltpu.make_async_copy(r3_ref.at[j, p], w3_sc.at[slot, :, sl], load_sems.at[slot, 1]))
             copies.append(pltpu.make_async_copy(r2_ref.at[j, p], w2_sc.at[slot, sl, :], load_sems.at[slot, 2]))
         return copies
+
+    def end_loads(slot):
+        w = e1_ref.shape[1]
+        return [
+            pltpu.make_async_copy(e1_ref, w1_sc.at[slot, :, pl.ds(0, w)], load_sems.at[slot, 0]),
+            pltpu.make_async_copy(e3_ref, w3_sc.at[slot, :, pl.ds(0, w)], load_sems.at[slot, 1]),
+            pltpu.make_async_copy(e2_ref, w2_sc.at[slot, pl.ds(0, w), :], load_sems.at[slot, 2]),
+        ]
 
     def compute(slot, lane_keep):
         def rows_step(m, carry):
@@ -466,6 +513,9 @@
     net.barrier()
     net.start(0, N_EARLY)
     net.start(0, N_EARLY + 1)
+    net.start(1, N_EARLY - 1)
+    net.start(2, N_EARLY - 1)
+    net.start(3, N_EARLY - 2)
     for copy in own_loads(0, 0):
         copy.start()
 
@@ -475,34 +525,31 @@
         attn = attn + jnp.dot(o_ref[1, sl, :], ro_ref[...], preferred_element_type=jnp.float32)
         residual = (x_ref[sl, :].astype(jnp.float32) + attn).astype(jnp.bfloat16).astype(jnp.float32)
         acc_sc[sl, :] = residual
-        b_ref[sl, :] = normed_rows(residual, gain_ref[...].astype(jnp.float32))
+        b_ref[sl, :] = normed_rows(residual, gain_ref[...].astype(jnp.float32)[None, :])
         return carry
 
     lax.fori_loop(0, x_ref.shape[0] // Q_ROWS, residual_rows, 0)
     lane_tile = lax.broadcasted_iota(jnp.int32, (1, width), 1) // TILE
-    source = 2 * lax.rem(lane_tile + net.c // 2, 2) + lax.rem(lane_tile // 2 + lax.rem(net.c, 2), 2)
 
     def pass_on(s, forward, second):
         for when, chunks in forward.items():
             @pl.when(s == when)
             def _(chunks=chunks):
                 for j in chunks:
-                    if j >= N_EARLY:
-                        net.arrived(0, j)
-                    net.start(1, j)
-                    net.start(2, j)
-                    if N_EARLY + 2 <= j + 2 < N_CHUNKS:
+                    net.pass_on(j)
+                    if j + 2 < N_CHUNKS - 1:
                         net.start(0, j + 2)
+                    elif j + 2 == N_CHUNKS - 1:
+                        for copy in net.last_chunk(0, ends):
+                            copy.start()
         for when, chunks in second.items():
             @pl.when(s == when)
             def _(chunks=chunks):
                 for j in chunks:
-                    if j >= 4:
-                        net.arrived(1, j)
-                    net.start(3, j)
+                    net.pass_second(j)
 
     def load_next(s, slot, after):
-        for j in range(3, N_CHUNKS):
+        for j in range(3, N_CHUNKS - 1):
             if (N_CHUNKS - 1 + j >= LOAD_AFTER) == after:
                 @pl.when(s == N_CHUNKS - 1 + j)
                 def _(j=j):
@@ -516,7 +563,18 @@
                 for copy in own_loads(s + 1, 1 - slot):
                     copy.start()
 
-        first, last = (LOAD_AFTER, 2 * N_CHUNKS - 1) if after else (N_CHUNKS - 1, LOAD_AFTER)
+        if after:
+            @pl.when(s == 2 * N_CHUNKS - 2)
+            def _():
+                for copy, on in zip(net.last_chunk(0, ends), net.last_chunk(2, ends)):
+                    copy.wait_recv()
+                    on.start()
+                for on in net.last_chunk(2, ends):
+                    on.wait_recv()
+                for copy in end_loads(1 - slot):
+                    copy.start()
+
+        first, last = (LOAD_AFTER, 2 * N_CHUNKS - 2) if after else (N_CHUNKS - 1, LOAD_AFTER)
 
         @pl.when((s >= first) & (s < last))
         def _():
@@ -527,11 +585,19 @@
         slot = lax.rem(s, 2)
         pass_on(s, LATE_FORWARD, LATE_SECOND)
         load_next(s, slot, False)
-        for copy in own_loads(0, slot):
-            copy.wait()
+        @pl.when(s < 2 * N_CHUNKS - 1)
+        def _():
+            for copy in own_loads(0, slot):
+                copy.wait()
+
+        @pl.when(s == 2 * N_CHUNKS - 1)
+        def _():
+            for copy in end_loads(slot):
+                copy.wait()
+
         own_end = (s == N_CHUNKS - 1).astype(jnp.float32)
         other_end = (s == 2 * N_CHUNKS - 1).astype(jnp.float32)
-        keep = 1.0 - own_end * (lane_tile == 0).astype(jnp.float32) - other_end * (source == 3).astype(jnp.float32)
+        keep = 1.0 - own_end * (lane_tile == 0).astype(jnp.float32) - other_end * (lane_tile == 3).astype(jnp.float32)
         compute(slot, keep)
         pass_on(s, END_FORWARD, END_SECOND)
         load_next(s, slot, True)
@@ -539,13 +605,16 @@
 
     lax.fori_loop(0, 2 * N_CHUNKS, step, 0)
     out_ref[...] = acc_sc[...].astype(out_ref.dtype)
-    for j in range(N_EARLY, N_CHUNKS):
+    for j in range(N_EARLY, N_CHUNKS - 1):
         net.sent(0, j)
-    for j in range(4, N_CHUNKS):
+    for j in range(N_EARLY - 1, N_CHUNKS - 1):
         net.sent(1, j)
         net.sent(2, j)
-    for j in range(3, N_CHUNKS):
+    for j in range(N_EARLY - 2, N_CHUNKS - 1):
         net.sent(3, j)
+    for stage in (0, 2):
+        for copy in net.last_chunk(stage, ends):
+            copy.wait_send()
 
 
 def mlp(x, gain, o, wo, ro, w1, w3, w2, early):
@@ -554,12 +623,13 @@
     hbm = pl.BlockSpec(memory_space=pl.ANY)
     bf16 = jnp.bfloat16
     width = 4 * TILE
+    left = w1.shape[1] % width
     n = N_CHUNKS
     return pl.pallas_call(
         mlp_kernel,
         in_specs=[vm] * 5 + [hbm] * 6,
-        out_specs=[vm, hbm, hbm, hbm],
-        out_shape=[jax.ShapeDtypeStruct((rows, dim), bf16)] + [jax.ShapeDtypeStruct(a.shape, bf16) for a in early],
+        out_specs=[vm] + [hbm] * 6,
+        out_shape=[jax.ShapeDtypeStruct((rows, dim), bf16)] + [jax.ShapeDtypeStruct(a.shape, bf16) for a in early] + [jax.ShapeDtypeStruct(s, bf16) for s in ((dim, left), (dim, left), (left, dim))],
         input_output_aliases={8: 1, 9: 2, 10: 3},
         scratch_shapes=[
             pltpu.VMEM((2, dim, width), bf16),
@@ -584,14 +654,11 @@
         local_q, head_dim = w_query.shape[1], w_query.shape[2]
         cp_index = lax.axis_index("cp")
         piece = jnp.where(lax.axis_index("tp") == 0, cp_index, n_pieces - 1 - cp_index)
-        cosine, sine_tab = rope_tables(piece * tok_dev + jnp.arange(tok_dev, dtype=jnp.int32), head_dim)
-        cos2 = jnp.concatenate([cosine, cosine], axis=1)
-        sin2 = jnp.concatenate([-sine_tab, sine_tab], axis=1)
-        wq = w_query.reshape(dim, local_q * head_dim)
-        wkv = jnp.concatenate([w_key.reshape(dim, -1), w_value.reshape(dim, -1)], axis=1)
+        cos2, sin2 = rope_tables(piece * tok_dev + jnp.arange(tok_dev, dtype=jnp.int32), head_dim)
+        wq, wk, wv = (jnp.transpose(w, (1, 0, 2)) for w in (w_query, w_key, w_value))
         wo = w_out.reshape(local_q * head_dim, dim)
-        o, k_cache, v_cache, wo_other, *early = attention(x_loc, norm_attn[None], cos2, sin2, wq, wkv, wo, w_gate, w_up, w_down)
-        layer_out = mlp(x_loc, norm_mlp[None], o, wo, wo_other, w_gate, w_up, w_down, early)
+        o, k_cache, v_cache, wo_other, *early = attention(x_loc, norm_attn, cos2, sin2, wq, wk, wv, wo, w_gate, w_up, w_down)
+        layer_out = mlp(x_loc, norm_mlp, o, wo, wo_other, w_gate, w_up, w_down, early)
         return layer_out, k_cache, v_cache
 
     row_spec = P(("dp", "cp", "tp"), None)

time: 376 us -> 350 us (0.931)
  Pallas kernels: 354 us -> 334 us
  local copies, waits for them, and re-layouts: 13.3 us -> 5.44 us
    pallas_call x2, Pallas kernels: 354 us -> 334 us  [the longest x1 196 us: attention(): pl.pallas_call(attention_kernel, in_specs=[vm] * 7 + [hbm] * 4, out_specs...]
    unnamed x8 -> x7, local copies, waits for them, and re-layouts: 8.27 us -> 5.44 us
where the time goes in v3:
time: 350 us; the launch traced here: 343 us
  Pallas kernels  334 us (95%)
  local copies, waits for them, and re-layouts  5.44 us (2%)
    pallas_call x1, Pallas kernels, attention(): pl.pallas_call(attention_kernel, in_specs=[vm] * 7 + [hbm] * 4, out_specs...  196 us
    pallas_call x1, Pallas kernels, mlp(): pl.pallas_call(mlp_kernel, in_specs=[vm] * 5 + [hbm] * 6, out_specs=[vm]...  138 us

profile of v3, /device:TPU:5, one launch (start us, length us, event | category | flops | bytes accessed | tf_op | source)
XLA Modules:
  0.0 343.3 jit_solution(1657431891330485253)
XLA Ops:
  0.7 3.1 negate_select_fusion
  3.8 195.9 %attention.1 = (bf16[2,1024,768]{2,1,0:T(8,128)(2,1)}, bf16[2048,128]{1,0:T(8,128)(2,1)}, bf16[2048,128]{1,0:T(8,128)(2,1)}, bf16[768,1536]{1,0:T(8,128)(2,1)}, ...) custom-call(bf16[1024,1536]{1,0:T(8,128)(2,1)} %x_ref.3, ...), custom_call_target="tpu_custom_call" | custom-call | flops 51539607552 | bytes 33554432 | tf_op jit(solution)/shard_map/attention/pallas_call | solution.py:421
  199.7 138.2 %mlp.1 = (bf16[1024,1536]{1,0:T(8,128)(2,1)}, bf16[8,4,1536,128]{3,2,1,0:T(8,128)(2,1)}, bf16[8,4,1536,128]{3,2,1,0:T(8,128)(2,1)}, bf16[8,4,128,1536]{3,2,1,0:T...) custom-call(bf16[1024,1536]{1,0:T(8,128)(2,1)} %x_ref.3, ...), custom_call_target="tpu_custom_call", output_to_operand_aliasing={{1}: (8, {}), {2}: (9, {}), {3}: (10, {})} | custom-call | flops 84557168640 | bytes 82575360 | tf_op jit(solution)/shard_map/mlp/pallas_call | solution.py:628
  337.9 0.0 copy-start.1
  337.9 0.0 copy-start
  337.9 3.8 %copy.22 = bf16[1024,1536]{1,0:T(8,128)(2,1)} copy(bf16[1024,1536]{1,0:T(8,128)(2,1)} %get-tuple-element.24) | data formatting | bytes 6291456
  341.7 0.0 copy-done.1
  341.7 0.8 copy.23
  342.5 0.0 copy-done
  342.5 0.8 copy.24
  (3 shorter events, 0.0 us)
Async XLA Ops:
  337.9 3.9 %copy-start.1 = (bf16[2048,128]{1,0:T(8,128)(2,1)S(1)}, bf16[2048,128]{1,0:T(8,128)(2,1)}, u32[]{:S(2)}) copy-start(bf16[2048,128]{1,0:T(8,128)(2,1)} %get-tuple-element.25) | copy-start | bytes 1572868
  337.9 4.7 %copy-start = (bf16[2048,128]{1,0:T(8,128)(2,1)S(1)}, bf16[2048,128]{1,0:T(8,128)(2,1)}, u32[]{:S(2)}) copy-start(bf16[2048,128]{1,0:T(8,128)(2,1)} %get-tuple-element.26) | copy-start | bytes 1572868

commit v4 on v3

--- a/solution.py
+++ b/solution.py
@@ -18,15 +18,12 @@
 TILE = 128
 N_CHUNKS = 9
 N_EARLY = 5
-
-
-def rope_tables(positions, head_dim):
-    half_dim = head_dim // 2
+PART = 1
+
+
+def rope_frequencies(head_dim):
     lane = jnp.arange(head_dim, dtype=jnp.int32)
-    inv_freq = ROPE_BASE ** (-2.0 * (lane % half_dim).astype(jnp.float32) / head_dim)
-    angles = positions.astype(jnp.float32)[:, None] * inv_freq[None, :]
-    sine_tab = jnp.sin(angles)
-    return jnp.cos(angles), jnp.where(lane < half_dim, -sine_tab, sine_tab)
+    return ROPE_BASE ** (-2.0 * (lane % (head_dim // 2)).astype(jnp.float32) / head_dim)
 
 
 class Links:
@@ -50,10 +47,10 @@
     def remote(self, src, dst, ssem, rsem, to):
         return pltpu.make_async_remote_copy(src_ref=src, dst_ref=dst, send_sem=ssem, recv_sem=rsem, device_id=self.peer[to], device_id_type=MESH)
 
-    def chunk(self, stage, j):
+    def chunk(self, stage, j, arrays=slice(0, 3)):
         to = "yxdd"[stage]
         copies = []
-        for a in range(3):
+        for a in range(3)[arrays]:
             if stage == 0:
                 tile = 4 * j + self.c
                 sl = pl.ds(pl.multiple_of(tile * TILE, TILE), TILE)
@@ -81,27 +78,28 @@
             copies.append(self.remote(src, dst, self.send_sems.at[j, stage, a], self.recv_sems.at[j, stage, a], "y.d"[stage]))
         return copies
 
-    def pass_on(self, j):
-        for first, over_x, over_d in zip(self.chunk(0, j), self.chunk(1, j), self.chunk(2, j)):
-            first.wait_recv()
-            over_x.start()
-            over_d.start()
+    def pass_on(self, j, here=0):
+        for a in range(3):
+            if a >= here:
+                self.arrived(0, j, slice(a, a + 1))
+            self.start(1, j, slice(a, a + 1))
+            self.start(2, j, slice(a, a + 1))
 
     def pass_second(self, j):
         for first, over_d in zip(self.chunk(1, j), self.chunk(3, j)):
             first.wait_recv()
             over_d.start()
 
-    def start(self, stage, j):
-        for copy in self.chunk(stage, j):
+    def start(self, stage, j, arrays=slice(0, 3)):
+        for copy in self.chunk(stage, j, arrays):
             copy.start()
 
-    def arrived(self, stage, j):
-        for copy in self.chunk(stage, j):
+    def arrived(self, stage, j, arrays=slice(0, 3)):
+        for copy in self.chunk(stage, j, arrays):
             copy.wait_recv()
 
-    def sent(self, stage, j):
-        for copy in self.chunk(stage, j):
+    def sent(self, stage, j, arrays=slice(0, 3)):
+        for copy in self.chunk(stage, j, arrays):
             copy.wait_send()
 
 
@@ -115,9 +113,9 @@
     return (wide * inv_rms * gain).astype(jnp.bfloat16)
 
 
-def attention_kernel(x_ref, gain_ref, cos_ref, sin_ref, wq_ref, wk_ref, wv_ref, wo_ref, w1_ref, w3_ref, w2_ref,
+def attention_kernel(x_ref, gain_ref, freq_ref, wq_ref, wk_ref, wv_ref, wo_ref, w1_ref, w3_ref, w2_ref,
                      o_ref, kc_ref, vc_ref, ro_ref, r1_ref, r3_ref, r2_ref,
-                     a_sc, q_sc, wq_sc, wk_sc, wv_sc, kv_buf, m_sc, l_sc, acc_sc, send_sems, recv_sems, kv_send, kv_recv, wt_send, wt_recv):
+                     cos_ref, sin_ref, a_sc, q_sc, wq_sc, wk_sc, wv_sc, kv_buf, m_sc, l_sc, acc_sc, send_sems, recv_sems, kv_send, kv_recv, wt_send, wt_recv):
     head_dim = 128
     half_dim = head_dim // 2
     chunk_len = x_ref.shape[0]
@@ -162,6 +160,11 @@
     def norm_x():
         def body(i, carry):
             sl = row_slice(i)
+            row = (y * (7 - 2 * c) + c) * chunk_len + i * Q_ROWS + lax.broadcasted_iota(jnp.int32, (Q_ROWS, head_dim), 0)
+            angles = row.astype(jnp.float32) * freq_ref[...][None, :]
+            sine_tab = jnp.sin(angles)
+            cos_ref[sl, :] = jnp.cos(angles)
+            sin_ref[sl, :] = jnp.where(lax.broadcasted_iota(jnp.int32, (Q_ROWS, head_dim), 1) < half_dim, -sine_tab, sine_tab)
             a_sc[sl, :] = normed_rows(x_ref[sl, :].astype(jnp.float32), gain_ref[...].astype(jnp.float32)[None, :])
             return carry
         lax.fori_loop(0, q_blocks, body, 0)
@@ -334,6 +337,8 @@
                 net.pass_on(j)
                 if j + 2 < N_EARLY:
                     net.start(0, j + 2)
+                elif j + 2 == N_EARLY:
+                    net.start(0, N_EARLY, slice(0, PART))
 
         for j, when in EARLY_SECOND:
             @pl.when(s == when)
@@ -398,6 +403,8 @@
         if j not in forwarded:
             net.arrived(0, j)
         net.sent(0, j)
+    net.arrived(0, N_EARLY, slice(0, PART))
+    net.sent(0, N_EARLY, slice(0, PART))
     for j in forwarded:
         if j not in second:
             net.arrived(1, j)
@@ -409,7 +416,7 @@
         net.sent(3, j)
 
 
-def attention(x, gain, cos2, sin2, wq, wk, wv, wo, w1, w3, w2):
+def attention(x, gain, freq, wq, wk, wv, wo, w1, w3, w2):
     rows, dim = x.shape
     width = wq.shape[0] * 128
     states = 2 * rows // Q_ROWS
@@ -417,10 +424,10 @@
     vm = pl.BlockSpec(memory_space=pltpu.VMEM)
     hbm = pl.BlockSpec(memory_space=pl.ANY)
     bf16 = jnp.bfloat16
-    n = N_EARLY
+    n = N_EARLY + 1
     return pl.pallas_call(
         attention_kernel,
-        in_specs=[vm] * 7 + [hbm] * 4,
+        in_specs=[vm] * 6 + [hbm] * 4,
         out_specs=[vm, vm, vm, hbm, hbm, hbm, hbm],
         out_shape=[
             jax.ShapeDtypeStruct((2, rows, width), bf16),
@@ -432,6 +439,8 @@
             jax.ShapeDtypeStruct((N_CHUNKS - 1, 4, TILE, dim), bf16),
         ],
         scratch_shapes=[
+            pltpu.VMEM((rows, 128), jnp.float32),
+            pltpu.VMEM((rows, 128), jnp.float32),
             pltpu.VMEM((rows, dim), bf16),
             pltpu.VMEM((2, rows, width), bf16),
             pltpu.VMEM(wq.shape, bf16),
@@ -451,7 +460,7 @@
         compiler_params=pltpu.CompilerParams(collective_id=0, has_side_effects=True, vmem_limit_bytes=VMEM_LIMIT),
         cost_estimate=pl.CostEstimate(flops=16 * rows * 4096 * width, bytes_accessed=32 * 2**20, transcendentals=rows * 4096 * 12),
         name="attention",
-    )(x, gain, cos2, sin2, wq, wk, wv, wo, w1, w3, w2)
+    )(x, gain, freq, wq, wk, wv, wo, w1, w3, w2)
 
 
 M_BLOCK = 512
@@ -505,13 +514,15 @@
             up = jnp.dot(b, w3_sc[slot], preferred_element_type=jnp.float32)
             hidden = jax.nn.silu(gate) * up
             hidden = jnp.where(lane_keep > 0.5, hidden, 0.0).astype(jnp.bfloat16)
-            acc_sc[sl, :] += jnp.dot(hidden, w2_sc[slot], preferred_element_type=jnp.float32)
+            total = acc_sc[sl, :] + jnp.dot(hidden, w2_sc[slot], preferred_element_type=jnp.float32)
+            acc_sc[sl, :] = total
+            out_ref[sl, :] = total.astype(out_ref.dtype)
             return carry
 
         lax.fori_loop(0, b_ref.shape[0] // M_BLOCK, rows_step, 0)
 
     net.barrier()
-    net.start(0, N_EARLY)
+    net.start(0, N_EARLY, slice(PART, 3))
     net.start(0, N_EARLY + 1)
     net.start(1, N_EARLY - 1)
     net.start(2, N_EARLY - 1)
@@ -536,7 +547,7 @@
             @pl.when(s == when)
             def _(chunks=chunks):
                 for j in chunks:
-                    net.pass_on(j)
+                    net.pass_on(j, PART if j == N_EARLY else 0)
                     if j + 2 < N_CHUNKS - 1:
                         net.start(0, j + 2)
                     elif j + 2 == N_CHUNKS - 1:
@@ -604,8 +615,8 @@
         return carry
 
     lax.fori_loop(0, 2 * N_CHUNKS, step, 0)
-    out_ref[...] = acc_sc[...].astype(out_ref.dtype)
-    for j in range(N_EARLY, N_CHUNKS - 1):
+    net.sent(0, N_EARLY, slice(PART, 3))
+    for j in range(N_EARLY + 1, N_CHUNKS - 1):
         net.sent(0, j)
     for j in range(N_EARLY - 1, N_CHUNKS - 1):
         net.sent(1, j)
@@ -647,17 +658,10 @@
     )(x, gain, o, wo, ro, w1, w3, w2, *early)[0]
 
 def solution(mesh):
-    n_pieces = 2 * mesh.shape["cp"]
-
     def layer_shard(x_loc, norm_attn, norm_mlp, w_query, w_key, w_value, w_out, w_gate, w_up, w_down):
-        tok_dev, dim = x_loc.shape
-        local_q, head_dim = w_query.shape[1], w_query.shape[2]
-        cp_index = lax.axis_index("cp")
-        piece = jnp.where(lax.axis_index("tp") == 0, cp_index, n_pieces - 1 - cp_index)
-        cos2, sin2 = rope_tables(piece * tok_dev + jnp.arange(tok_dev, dtype=jnp.int32), head_dim)
         wq, wk, wv = (jnp.transpose(w, (1, 0, 2)) for w in (w_query, w_key, w_value))
-        wo = w_out.reshape(local_q * head_dim, dim)
-        o, k_cache, v_cache, wo_other, *early = attention(x_loc, norm_attn, cos2, sin2, wq, wk, wv, wo, w_gate, w_up, w_down)
+        wo = w_out.reshape(-1, w_out.shape[2])
+        o, k_cache, v_cache, wo_other, *early = attention(x_loc, norm_attn, rope_frequencies(w_query.shape[2]), wq, wk, wv, wo, w_gate, w_up, w_down)
         layer_out = mlp(x_loc, norm_mlp, o, wo, wo_other, w_gate, w_up, w_down, early)
         return layer_out, k_cache, v_cache
 

time: 350 us -> 341 us (0.974); the launches traced: 343 us -> 338 us
  no operation moved by 1% of the time
where the time goes in v4:
time: 341 us; the launch traced here: 338 us
  Pallas kernels  332 us (97%)
  local copies, waits for them, and re-layouts  5.44 us (2%)
    pallas_call x1, Pallas kernels, attention(): pl.pallas_call(attention_kernel, in_specs=[vm] * 6 + [hbm] * 4, out_specs...  196 us
    pallas_call x1, Pallas kernels, mlp(): pl.pallas_call(mlp_kernel, in_specs=[vm] * 5 + [hbm] * 6, out_specs=[vm]...  136 us

profile of v4, /device:TPU:5, one launch (start us, length us, event | category | flops | bytes accessed | tf_op | source)
XLA Modules:
  0.0 338.3 jit_solution(16470941154754888030)
XLA Ops:
  0.6 0.5 fusion.2.freq_ref
  1.2 195.8 %attention.1 = (bf16[2,1024,768]{2,1,0:T(8,128)(2,1)}, bf16[2048,128]{1,0:T(8,128)(2,1)}, bf16[2048,128]{1,0:T(8,128)(2,1)}, bf16[768,1536]{1,0:T(8,128)(2,1)}, ...) custom-call(bf16[1024,1536]{1,0:T(8,128)(2,1)} %x_ref.3, ...), custom_call_target="tpu_custom_call" | custom-call | flops 51539607552 | bytes 33554432 | tf_op jit(solution)/shard_map/attention/pallas_call | solution.py:428
  196.9 135.9 %mlp.1 = (bf16[1024,1536]{1,0:T(8,128)(2,1)}, bf16[8,4,1536,128]{3,2,1,0:T(8,128)(2,1)}, bf16[8,4,1536,128]{3,2,1,0:T(8,128)(2,1)}, bf16[8,4,128,1536]{3,2,1,0:T...) custom-call(bf16[1024,1536]{1,0:T(8,128)(2,1)} %x_ref.3, ...), custom_call_target="tpu_custom_call", output_to_operand_aliasing={{1}: (8, {}), {2}: (9, {}), {3}: (10, {})} | custom-call | flops 84557168640 | bytes 82575360 | tf_op jit(solution)/shard_map/mlp/pallas_call | solution.py:639
  332.9 0.0 copy-start.1
  332.9 0.0 copy-start
  332.9 3.8 %copy.22 = bf16[1024,1536]{1,0:T(8,128)(2,1)} copy(bf16[1024,1536]{1,0:T(8,128)(2,1)} %get-tuple-element.22) | data formatting | bytes 6291456
  336.7 0.0 copy-done.1
  336.7 0.8 copy.23
  337.5 0.0 copy-done
  337.5 0.8 copy.24
Async XLA Ops:
  332.9 3.9 %copy-start.1 = (bf16[2048,128]{1,0:T(8,128)(2,1)S(1)}, bf16[2048,128]{1,0:T(8,128)(2,1)}, u32[]{:S(2)}) copy-start(bf16[2048,128]{1,0:T(8,128)(2,1)} %get-tuple-element.23) | copy-start | bytes 1572868
  332.9 4.7 %copy-start = (bf16[2048,128]{1,0:T(8,128)(2,1)S(1)}, bf16[2048,128]{1,0:T(8,128)(2,1)}, u32[]{:S(2)}) copy-start(bf16[2048,128]{1,0:T(8,128)(2,1)} %get-tuple-element.24) | copy-start | bytes 1572868

commit v5 on v4

--- a/solution.py
+++ b/solution.py
@@ -60,11 +60,11 @@
             copies.append(self.remote(src, self.recv[a].at[j, stage], self.send_sems.at[j, stage, a], self.recv_sems.at[j, stage, a], to))
         return copies
 
-    def last_chunk(self, stage, last):
+    def last_chunk(self, stage, last, arrays=slice(0, 3)):
         half = lax.rem(self.c, 2)
         begin = (self.n_tiles // 4) * 4 * TILE
         copies = []
-        for a in range(3):
+        for a in range(3)[arrays]:
             depth = last[a].shape[0] // 2
             at = pl.ds(pl.multiple_of(half * depth, 64), depth)
             dst = last[a].at[at, :]
@@ -103,8 +103,8 @@
             copy.wait_send()
 
 
-EARLY_FORWARD = ((0, 14), (1, 17), (2, 19), (3, 21))
-EARLY_SECOND = ((0, 18), (1, 20), (2, 22))
+EARLY_FORWARD = ((0, 15), (1, 18), (2, 20), (3, 22))
+EARLY_SECOND = ((0, 19), (1, 21), (2, 23))
 SLOT_SOURCE = (0, 0, 0, 1)
 
 
@@ -464,15 +464,15 @@
 
 
 M_BLOCK = 512
-LATE_FORWARD = {3: (5,), 7: (6,)}
-LATE_SECOND = {3: (4,), 8: (5,)}
-END_FORWARD = {12: (7,)}
-END_SECOND = {12: (6,), 15: (7,)}
-LOAD_AFTER = 12
+LATE_FORWARD = {3: (5,), 7: (6,), 11: (7,)}
+LATE_SECOND = {3: (4,), 8: (5,), 12: (6,)}
+END_SECOND = {15: (7,)}
+LOAD_AFTER = 15
+STEPS = 2 * N_CHUNKS - 1
 
 
 def mlp_kernel(x_ref, gain_ref, o_ref, wo_ref, ro_ref, w1_ref, w3_ref, w2_ref, a1_ref, a3_ref, a2_ref, out_ref, r1_ref, r3_ref, r2_ref, e1_ref, e3_ref, e2_ref,
-               w1_sc, w3_sc, w2_sc, b_ref, acc_sc, load_sems, send_sems, recv_sems):
+               w1_sc, w3_sc, w2_sc, b_ref, acc_sc, hid_sc, load_sems, send_sems, recv_sems):
     dim = x_ref.shape[1]
     width = 4 * TILE
     n_tiles = w1_ref.shape[1] // TILE
@@ -498,13 +498,10 @@
             copies.append(pltpu.make_async_copy(r2_ref.at[j, p], w2_sc.at[slot, sl, :], load_sems.at[slot, 2]))
         return copies
 
-    def end_loads(slot):
-        w = e1_ref.shape[1]
-        return [
-            pltpu.make_async_copy(e1_ref, w1_sc.at[slot, :, pl.ds(0, w)], load_sems.at[slot, 0]),
-            pltpu.make_async_copy(e3_ref, w3_sc.at[slot, :, pl.ds(0, w)], load_sems.at[slot, 1]),
-            pltpu.make_async_copy(e2_ref, w2_sc.at[slot, pl.ds(0, w), :], load_sems.at[slot, 2]),
-        ]
+    def end_load(slot, a):
+        w = pl.ds(0, e1_ref.shape[1])
+        dst = w2_sc.at[slot, w, :] if a == 2 else (w1_sc, w3_sc)[a].at[slot, :, w]
+        return pltpu.make_async_copy(ends[a], dst, load_sems.at[slot, a])
 
     def compute(slot, lane_keep):
         def rows_step(m, carry):
@@ -514,9 +511,7 @@
             up = jnp.dot(b, w3_sc[slot], preferred_element_type=jnp.float32)
             hidden = jax.nn.silu(gate) * up
             hidden = jnp.where(lane_keep > 0.5, hidden, 0.0).astype(jnp.bfloat16)
-            total = acc_sc[sl, :] + jnp.dot(hidden, w2_sc[slot], preferred_element_type=jnp.float32)
-            acc_sc[sl, :] = total
-            out_ref[sl, :] = total.astype(out_ref.dtype)
+            acc_sc[sl, :] += jnp.dot(hidden, w2_sc[slot], preferred_element_type=jnp.float32)
             return carry
 
         lax.fori_loop(0, b_ref.shape[0] // M_BLOCK, rows_step, 0)
@@ -574,18 +569,14 @@
                 for copy in own_loads(s + 1, 1 - slot):
                     copy.start()
 
-        if after:
-            @pl.when(s == 2 * N_CHUNKS - 2)
+        if not after:
+            @pl.when(s == STEPS - 1)
             def _():
-                for copy, on in zip(net.last_chunk(0, ends), net.last_chunk(2, ends)):
-                    copy.wait_recv()
-                    on.start()
-                for on in net.last_chunk(2, ends):
-                    on.wait_recv()
-                for copy in end_loads(1 - slot):
-                    copy.start()
-
-        first, last = (LOAD_AFTER, 2 * N_CHUNKS - 2) if after else (N_CHUNKS - 1, LOAD_AFTER)
+                for a in range(2):
+                    net.last_chunk(2, ends, slice(a, a + 1))[0].wait_recv()
+                    end_load(1 - slot, a).start()
+
+        first, last = (LOAD_AFTER, STEPS - 1) if after else (N_CHUNKS - 1, LOAD_AFTER)
 
         @pl.when((s >= first) & (s < last))
         def _():
@@ -596,25 +587,50 @@
         slot = lax.rem(s, 2)
         pass_on(s, LATE_FORWARD, LATE_SECOND)
         load_next(s, slot, False)
-        @pl.when(s < 2 * N_CHUNKS - 1)
-        def _():
-            for copy in own_loads(0, slot):
-                copy.wait()
-
-        @pl.when(s == 2 * N_CHUNKS - 1)
-        def _():
-            for copy in end_loads(slot):
-                copy.wait()
-
-        own_end = (s == N_CHUNKS - 1).astype(jnp.float32)
-        other_end = (s == 2 * N_CHUNKS - 1).astype(jnp.float32)
-        keep = 1.0 - own_end * (lane_tile == 0).astype(jnp.float32) - other_end * (lane_tile == 3).astype(jnp.float32)
+        for copy in own_loads(0, slot):
+            copy.wait()
+
+        keep = 1.0 - (s == N_CHUNKS - 1).astype(jnp.float32) * (lane_tile == 0).astype(jnp.float32)
         compute(slot, keep)
-        pass_on(s, END_FORWARD, END_SECOND)
+        pass_on(s, {}, END_SECOND)
+
+        @pl.when(s == STEPS - 2)
+        def _():
+            for a in range(2):
+                net.last_chunk(0, ends, slice(a, a + 1))[0].wait_recv()
+                net.last_chunk(2, ends, slice(a, a + 1))[0].start()
+
         load_next(s, slot, True)
         return carry
 
-    lax.fori_loop(0, 2 * N_CHUNKS, step, 0)
+    lax.fori_loop(0, STEPS, step, 0)
+
+    slot = STEPS % 2
+    left = e1_ref.shape[1]
+    net.last_chunk(0, ends, slice(2, 3))[0].wait_recv()
+    net.last_chunk(2, ends, slice(2, 3))[0].start()
+    for a in range(2):
+        end_load(slot, a).wait()
+
+    def hidden_rows(m, carry):
+        sl = pl.ds(pl.multiple_of(m * M_BLOCK, M_BLOCK), M_BLOCK)
+        gate = jnp.dot(b_ref[sl, :], w1_sc[slot, :, :left], preferred_element_type=jnp.float32)
+        up = jnp.dot(b_ref[sl, :], w3_sc[slot, :, :left], preferred_element_type=jnp.float32)
+        hid_sc[sl, :] = (jax.nn.silu(gate) * up).astype(jnp.bfloat16)
+        return carry
+
+    lax.fori_loop(0, x_ref.shape[0] // M_BLOCK, hidden_rows, 0)
+    net.last_chunk(2, ends, slice(2, 3))[0].wait_recv()
+    end_load(slot, 2).start()
+    end_load(slot, 2).wait()
+
+    def out_rows(m, carry):
+        sl = pl.ds(pl.multiple_of(m * M_BLOCK, M_BLOCK), M_BLOCK)
+        total = acc_sc[sl, :] + jnp.dot(hid_sc[sl, :], w2_sc[slot, :left, :], preferred_element_type=jnp.float32)
+        out_ref[sl, :] = total.astype(out_ref.dtype)
+        return carry
+
+    lax.fori_loop(0, x_ref.shape[0] // M_BLOCK, out_rows, 0)
     net.sent(0, N_EARLY, slice(PART, 3))
     for j in range(N_EARLY + 1, N_CHUNKS - 1):
         net.sent(0, j)
@@ -648,6 +664,7 @@
             pltpu.VMEM((2, width, dim), bf16),
             pltpu.VMEM((rows, dim), bf16),
             pltpu.VMEM((rows, dim), jnp.float32),
+            pltpu.VMEM((rows, left), bf16),
             pltpu.SemaphoreType.DMA((2, 3)),
             pltpu.SemaphoreType.DMA((n, 4, 3)),
             pltpu.SemaphoreType.DMA((n, 4, 3)),

time: 341 us -> 332 us (0.974)
  Pallas kernels: 332 us -> 326 us
    pallas_call x1, Pallas kernels: 136 us -> 131 us  [mlp(): pl.pallas_call(mlp_kernel, in_specs=[vm] * 5 + [hbm] * 6, out_specs=[vm]...]
where the time goes in v5:
time: 332 us
  Pallas kernels  326 us (98%)
  local copies, waits for them, and re-layouts  5.44 us (2%)
    pallas_call x1, Pallas kernels, attention(): pl.pallas_call(attention_kernel, in_specs=[vm] * 6 + [hbm] * 4, out_specs...  195 us
    pallas_call x1, Pallas kernels, mlp(): pl.pallas_call(mlp_kernel, in_specs=[vm] * 5 + [hbm] * 6, out_specs=[vm]...  131 us

profile of v5, /device:TPU:5, one launch (start us, length us, event | category | flops | bytes accessed | tf_op | source)
XLA Modules:
  0.0 332.3 jit_solution(133633496343221840)
XLA Ops:
  0.6 0.5 fusion.2.freq_ref
  1.2 195.1 %attention.1 = (bf16[2,1024,768]{2,1,0:T(8,128)(2,1)}, bf16[2048,128]{1,0:T(8,128)(2,1)}, bf16[2048,128]{1,0:T(8,128)(2,1)}, bf16[768,1536]{1,0:T(8,128)(2,1)}, ...) custom-call(bf16[1024,1536]{1,0:T(8,128)(2,1)} %x_ref.3, ...), custom_call_target="tpu_custom_call" | custom-call | flops 51539607552 | bytes 33554432 | tf_op jit(solution)/shard_map/attention/pallas_call | solution.py:428
  196.3 130.6 %mlp.1 = (bf16[1024,1536]{1,0:T(8,128)(2,1)}, bf16[8,4,1536,128]{3,2,1,0:T(8,128)(2,1)}, bf16[8,4,1536,128]{3,2,1,0:T(8,128)(2,1)}, bf16[8,4,128,1536]{3,2,1,0:T...) custom-call(bf16[1024,1536]{1,0:T(8,128)(2,1)} %x_ref.3, ...), custom_call_target="tpu_custom_call", output_to_operand_aliasing={{1}: (8, {}), {2}: (9, {}), {3}: (10, {})} | custom-call | flops 84557168640 | bytes 82575360 | tf_op jit(solution)/shard_map/mlp/pallas_call | solution.py:655
  326.9 0.0 copy-start.1
  326.9 0.0 copy-start
  326.9 3.8 %copy.22 = bf16[1024,1536]{1,0:T(8,128)(2,1)} copy(bf16[1024,1536]{1,0:T(8,128)(2,1)} %get-tuple-element.22) | data formatting | bytes 6291456
  330.7 0.0 copy-done.1
  330.7 0.8 copy.23
  331.5 0.0 copy-done
  331.5 0.8 copy.24
Async XLA Ops:
  326.9 3.9 %copy-start.1 = (bf16[2048,128]{1,0:T(8,128)(2,1)S(1)}, bf16[2048,128]{1,0:T(8,128)(2,1)}, u32[]{:S(2)}) copy-start(bf16[2048,128]{1,0:T(8,128)(2,1)} %get-tuple-element.23) | copy-start | bytes 1572868
  326.9 4.7 %copy-start = (bf16[2048,128]{1,0:T(8,128)(2,1)S(1)}, bf16[2048,128]{1,0:T(8,128)(2,1)}, u32[]{:S(2)}) copy-start(bf16[2048,128]{1,0:T(8,128)(2,1)} %get-tuple-element.24) | copy-start | bytes 1572868

commit v6 on v5

--- a/solution.py
+++ b/solution.py
@@ -52,9 +52,12 @@
         copies = []
         for a in range(3)[arrays]:
             if stage == 0:
-                tile = 4 * j + self.c
-                sl = pl.ds(pl.multiple_of(tile * TILE, TILE), TILE)
-                src = self.weights[a].at[sl, :] if a == 2 else self.weights[a].at[:, sl]
+                w = self.weights[a]
+                if a == 2:
+                    src = w.at[pl.ds(pl.multiple_of((4 * j + self.c) * TILE, TILE), TILE), :]
+                else:
+                    depth = w.shape[0] // 4
+                    src = w.at[pl.ds(pl.multiple_of(self.c * depth, TILE), depth), pl.ds(4 * j * TILE, 4 * TILE)]
             else:
                 src = self.recv[a].at[j, (0, 0, 0, 1)[stage]]
             copies.append(self.remote(src, self.recv[a].at[j, stage], self.send_sems.at[j, stage, a], self.recv_sems.at[j, stage, a], to))
@@ -434,8 +437,8 @@
             jax.ShapeDtypeStruct((2 * rows, 128), bf16),
             jax.ShapeDtypeStruct((2 * rows, 128), bf16),
             jax.ShapeDtypeStruct(wo.shape, bf16),
-            jax.ShapeDtypeStruct((N_CHUNKS - 1, 4, dim, TILE), bf16),
-            jax.ShapeDtypeStruct((N_CHUNKS - 1, 4, dim, TILE), bf16),
+            jax.ShapeDtypeStruct((N_CHUNKS - 1, 4, dim // 4, 4 * TILE), bf16),
+            jax.ShapeDtypeStruct((N_CHUNKS - 1, 4, dim // 4, 4 * TILE), bf16),
             jax.ShapeDtypeStruct((N_CHUNKS - 1, 4, TILE, dim), bf16),
         ],
         scratch_shapes=[
@@ -471,8 +474,8 @@
 STEPS = 2 * N_CHUNKS - 1
 
 
-def mlp_kernel(x_ref, gain_ref, o_ref, wo_ref, ro_ref, w1_ref, w3_ref, w2_ref, a1_ref, a3_ref, a2_ref, out_ref, r1_ref, r3_ref, r2_ref, e1_ref, e3_ref, e2_ref,
-               w1_sc, w3_sc, w2_sc, b_ref, acc_sc, hid_sc, load_sems, send_sems, recv_sems):
+def mlp_kernel(x_ref, gain_ref, o_ref, wo_ref, ro_ref, w1_ref, w3_ref, w2_ref, a1_ref, a3_ref, a2_ref, out_ref, hid_ref, r1_ref, r3_ref, r2_ref, e1_ref, e3_ref, e2_ref,
+               w1_sc, w3_sc, w2_sc, b_ref, acc_sc, hid_sc, load_sems, store_sems, send_sems, recv_sems):
     dim = x_ref.shape[1]
     width = 4 * TILE
     n_tiles = w1_ref.shape[1] // TILE
@@ -491,10 +494,13 @@
 
     def other_loads(j, slot):
         copies = []
+        depth = dim // 4
         for p in range(4):
-            sl = pl.ds(p * TILE, TILE)
-            copies.append(pltpu.make_async_copy(r1_ref.at[j, p], w1_sc.at[slot, :, sl], load_sems.at[slot, 0]))
-            copies.append(pltpu.make_async_copy(r3_ref.at[j, p], w3_sc.at[slot, :, sl], load_sems.at[slot, 1]))
+            source = 2 * lax.rem(net.c // 2 + p % 2, 2) + lax.rem(net.c + p // 2, 2)
+            deep = pl.ds(pl.multiple_of(source * depth, TILE), depth)
+            sl = pl.ds(pl.multiple_of(source * TILE, TILE), TILE)
+            copies.append(pltpu.make_async_copy(r1_ref.at[j, p], w1_sc.at[slot, deep, :], load_sems.at[slot, 0]))
+            copies.append(pltpu.make_async_copy(r3_ref.at[j, p], w3_sc.at[slot, deep, :], load_sems.at[slot, 1]))
             copies.append(pltpu.make_async_copy(r2_ref.at[j, p], w2_sc.at[slot, sl, :], load_sems.at[slot, 2]))
         return copies
 
@@ -605,6 +611,8 @@
 
     lax.fori_loop(0, STEPS, step, 0)
 
+    store_sum = pltpu.make_async_copy(acc_sc, out_ref, store_sems.at[0])
+    store_sum.start()
     slot = STEPS % 2
     left = e1_ref.shape[1]
     net.last_chunk(0, ends, slice(2, 3))[0].wait_recv()
@@ -620,17 +628,11 @@
         return carry
 
     lax.fori_loop(0, x_ref.shape[0] // M_BLOCK, hidden_rows, 0)
+    store_hidden = pltpu.make_async_copy(hid_sc, hid_ref, store_sems.at[1])
+    store_hidden.start()
     net.last_chunk(2, ends, slice(2, 3))[0].wait_recv()
-    end_load(slot, 2).start()
-    end_load(slot, 2).wait()
-
-    def out_rows(m, carry):
-        sl = pl.ds(pl.multiple_of(m * M_BLOCK, M_BLOCK), M_BLOCK)
-        total = acc_sc[sl, :] + jnp.dot(hid_sc[sl, :], w2_sc[slot, :left, :], preferred_element_type=jnp.float32)
-        out_ref[sl, :] = total.astype(out_ref.dtype)
-        return carry
-
-    lax.fori_loop(0, x_ref.shape[0] // M_BLOCK, out_rows, 0)
+    store_sum.wait()
+    store_hidden.wait()
     net.sent(0, N_EARLY, slice(PART, 3))
     for j in range(N_EARLY + 1, N_CHUNKS - 1):
         net.sent(0, j)
@@ -655,9 +657,9 @@
     return pl.pallas_call(
         mlp_kernel,
         in_specs=[vm] * 5 + [hbm] * 6,
-        out_specs=[vm] + [hbm] * 6,
-        out_shape=[jax.ShapeDtypeStruct((rows, dim), bf16)] + [jax.ShapeDtypeStruct(a.shape, bf16) for a in early] + [jax.ShapeDtypeStruct(s, bf16) for s in ((dim, left), (dim, left), (left, dim))],
-        input_output_aliases={8: 1, 9: 2, 10: 3},
+        out_specs=[hbm] * 8,
+        out_shape=[jax.ShapeDtypeStruct((rows, dim), jnp.float32), jax.ShapeDtypeStruct((rows, left), bf16)] + [jax.ShapeDtypeStruct(a.shape, bf16) for a in early] + [jax.ShapeDtypeStruct(s, bf16) for s in ((dim, left), (dim, left), (left, dim))],
+        input_output_aliases={8: 2, 9: 3, 10: 4},
         scratch_shapes=[
             pltpu.VMEM((2, dim, width), bf16),
             pltpu.VMEM((2, dim, width), bf16),
@@ -666,21 +668,47 @@
             pltpu.VMEM((rows, dim), jnp.float32),
             pltpu.VMEM((rows, left), bf16),
             pltpu.SemaphoreType.DMA((2, 3)),
+            pltpu.SemaphoreType.DMA((2,)),
             pltpu.SemaphoreType.DMA((n, 4, 3)),
             pltpu.SemaphoreType.DMA((n, 4, 3)),
         ],
         compiler_params=pltpu.CompilerParams(collective_id=1, has_side_effects=True, vmem_limit_bytes=VMEM_LIMIT),
         cost_estimate=pl.CostEstimate(flops=12 * rows * dim * w1.shape[1], bytes_accessed=12 * dim * w1.shape[1], transcendentals=2 * rows * w1.shape[1]),
         name="mlp",
-    )(x, gain, o, wo, ro, w1, w3, w2, *early)[0]
+    )(x, gain, o, wo, ro, w1, w3, w2, *early)
+
+
+def last_kernel(sum_ref, hid_ref, w2_ref, kc_ref, vc_ref, out_ref, k_ref, v_ref):
+    out_ref[...] = (sum_ref[...] + jnp.dot(hid_ref[...], w2_ref[...], preferred_element_type=jnp.float32)).astype(out_ref.dtype)
+    k_ref[...] = kc_ref[...]
+    v_ref[...] = vc_ref[...]
+
+
+def last_product(total, hidden, w2, k_cache, v_cache):
+    rows, dim = total.shape
+    steps = rows // Q_ROWS
+
+    def by_rows(a):
+        return pl.BlockSpec((a.shape[0] // steps, a.shape[1]), lambda i: (i, 0))
+
+    out = jax.ShapeDtypeStruct((rows, dim), jnp.bfloat16)
+    return pl.pallas_call(
+        last_kernel,
+        grid=(steps,),
+        in_specs=[by_rows(total), by_rows(hidden), pl.BlockSpec(w2.shape, lambda i: (0, 0)), by_rows(k_cache), by_rows(v_cache)],
+        out_specs=[by_rows(out), by_rows(k_cache), by_rows(v_cache)],
+        out_shape=[out, jax.ShapeDtypeStruct(k_cache.shape, k_cache.dtype), jax.ShapeDtypeStruct(v_cache.shape, v_cache.dtype)],
+        cost_estimate=pl.CostEstimate(flops=2 * rows * dim * w2.shape[0], bytes_accessed=6 * rows * dim, transcendentals=0),
+        name="last_product",
+    )(total, hidden, w2, k_cache, v_cache)
 
 def solution(mesh):
     def layer_shard(x_loc, norm_attn, norm_mlp, w_query, w_key, w_value, w_out, w_gate, w_up, w_down):
         wq, wk, wv = (jnp.transpose(w, (1, 0, 2)) for w in (w_query, w_key, w_value))
         wo = w_out.reshape(-1, w_out.shape[2])
         o, k_cache, v_cache, wo_other, *early = attention(x_loc, norm_attn, rope_frequencies(w_query.shape[2]), wq, wk, wv, wo, w_gate, w_up, w_down)
-        layer_out = mlp(x_loc, norm_mlp, o, wo, wo_other, w_gate, w_up, w_down, early)
-        return layer_out, k_cache, v_cache
+        total, hidden, *_, last_w2 = mlp(x_loc, norm_mlp, o, wo, wo_other, w_gate, w_up, w_down, early)
+        return tuple(last_product(total, hidden, last_w2, k_cache, v_cache))
 
     row_spec = P(("dp", "cp", "tp"), None)
     cache_spec = P(("dp", "cp"), "tp")

time: 332 us -> 330 us (level)
  local copies, waits for them, and re-layouts: 5.44 us -> 0 us
    unnamed x7 -> x0, local copies, waits for them, and re-layouts: 5.44 us -> none
    pallas_call x1 -> x2, Pallas kernels: 131 us -> 134 us  [the longest x1 126 us: mlp(): pl.pallas_call(mlp_kernel, in_specs=[vm] * 5 + [hbm] * 6, out_specs=[hbm]...]
where the time goes in v6:
time: 330 us
  Pallas kernels  329 us (100%)
    pallas_call x1, Pallas kernels, attention(): pl.pallas_call(attention_kernel, in_specs=[vm] * 6 + [hbm] * 4, out_specs...  195 us
    pallas_call x1, Pallas kernels, mlp(): pl.pallas_call(mlp_kernel, in_specs=[vm] * 5 + [hbm] * 6, out_specs=[hbm]...  126 us
    pallas_call x1, Pallas kernels, last_product(): pl.pallas_call(last_kernel, grid=(steps,), in_specs=[by_rows(total), by_r...  7.41 us

profile of v6, /device:TPU:5, one launch (start us, length us, event | category | flops | bytes accessed | tf_op | source)
XLA Modules:
  0.0 330.2 jit_solution(2494409799390457521)
XLA Ops:
  0.6 0.5 fusion.2.freq_ref
  1.2 195.1 %attention.1 = (bf16[2,1024,768]{2,1,0:T(8,128)(2,1)}, bf16[2048,128]{1,0:T(8,128)(2,1)}, bf16[2048,128]{1,0:T(8,128)(2,1)}, bf16[768,1536]{1,0:T(8,128)(2,1)}, ...) custom-call(bf16[1024,1536]{1,0:T(8,128)(2,1)} %x_ref.3, ...), custom_call_target="tpu_custom_call" | custom-call | flops 51539607552 | bytes 33554432 | tf_op jit(solution)/shard_map/attention/pallas_call | solution.py:431
  196.3 126.5 %mlp.1 = (f32[1024,1536]{1,0:T(8,128)}, bf16[1024,384]{1,0:T(8,128)(2,1)}, bf16[8,4,384,512]{3,2,1,0:T(8,128)(2,1)}, bf16[8,4,384,512]{3,2,1,0:T(8,128)(2,1)}, b...) custom-call(bf16[1024,1536]{1,0:T(8,128)(2,1)} %x_ref.3, ...), custom_call_target="tpu_custom_call", output_to_operand_aliasing={{2}: (8, {}), {3}: (9, {}), {4}: (10, {})} | custom-call | flops 84557168640 | bytes 82575360 | tf_op jit(solution)/shard_map/mlp/pallas_call | solution.py:657
  322.7 7.4 %last_product.1 = (bf16[1024,1536]{1,0:T(8,128)(2,1)}, bf16[2048,128]{1,0:T(8,128)(2,1)}, bf16[2048,128]{1,0:T(8,128)(2,1)}) custom-call(f32[1024,1536]{1,0:T(8,128)} %get-tuple-element.18.sum_ref, bf16[1024,384]{1,0:T(8,128)(2,1)} %get-tuple-element.19.hid_ref, bf16[384,1536]{1,0:T(8,128)(2,1)} %get-tuple-element.20.w2_ref, ...), custom_call_target="tpu_custom_call" | custom-call | flops 1207959552 | bytes 9437184 | tf_op jit(solution)/shard_map/last_product/pallas_call | solution.py:695

commit v7 on v6

--- a/solution.py
+++ b/solution.py
@@ -116,9 +116,9 @@
     return (wide * inv_rms * gain).astype(jnp.bfloat16)
 
 
-def attention_kernel(x_ref, gain_ref, freq_ref, wq_ref, wk_ref, wv_ref, wo_ref, w1_ref, w3_ref, w2_ref,
-                     o_ref, kc_ref, vc_ref, ro_ref, r1_ref, r3_ref, r2_ref,
-                     cos_ref, sin_ref, a_sc, q_sc, wq_sc, wk_sc, wv_sc, kv_buf, m_sc, l_sc, acc_sc, send_sems, recv_sems, kv_send, kv_recv, wt_send, wt_recv):
+def attention_kernel(x_hbm, gain_ref, freq_ref, wq_hbm, wk_hbm, wv_hbm, wo_ref, w1_ref, w3_ref, w2_ref,
+                     o_hbm, kc_ref, vc_ref, ro_ref, r1_ref, r3_ref, r2_ref,
+                     x_ref, wq_ref, wk_ref, wv_ref, o_ref, local_sems, cos_ref, sin_ref, a_sc, q_sc, wq_sc, wk_sc, wv_sc, kv_buf, m_sc, l_sc, acc_sc, send_sems, recv_sems, kv_send, kv_recv, wt_send, wt_recv):
     head_dim = 128
     half_dim = head_dim // 2
     chunk_len = x_ref.shape[0]
@@ -139,7 +139,7 @@
         return net.remote(kv_buf.at[src, hd], kv_buf.at[dst, hd], kv_send.at[n, hd], kv_recv.at[n, hd], to)
 
     def weight_copy(kind, stage):
-        own, held = ((wk_ref, wk_sc), (wv_ref, wv_sc), (wq_ref, wq_sc), (wo_ref, ro_ref))[kind]
+        own, held = ((wk_hbm, wk_sc), (wv_hbm, wv_sc), (wq_hbm, wq_sc), (wo_ref, ro_ref))[kind]
         quarter = own.shape[-2] // 4
         sl = pl.ds(pl.multiple_of((other_chip if stage == 3 else c) * quarter, 64), quarter)
         src = own if stage == 0 else held
@@ -193,9 +193,15 @@
             return carry
         lax.fori_loop(0, q_blocks, body, 0)
 
+    loads = [pltpu.make_async_copy(*pair, local_sems.at[n]) for n, pair in enumerate(((x_hbm, x_ref), (wk_hbm, wk_ref), (wv_hbm, wv_ref), (wq_hbm, wq_ref)))]
+    for load in loads:
+        load.start()
     net.barrier()
     weights_start((0, 1, 2), 0)
+    loads[0].wait()
     norm_x()
+    loads[1].wait()
+    loads[2].wait()
     make_kv(wk_ref, wv_ref, 0)
     m_sc[...] = jnp.full_like(m_sc, MASK_VALUE)
     l_sc[...] = jnp.zeros_like(l_sc)
@@ -206,6 +212,7 @@
     kv_copy(1, 0).start()
     kv_copy(0, 0).start()
     kv_copy(3, 0).start()
+    loads[3].wait()
     make_q(wq_ref, 0)
 
     def block(q_parts, state, start, slot, head, off, masked):
@@ -384,16 +391,22 @@
 
     lax.fori_loop(0, 2 * q_blocks, finish, 0)
 
+    stores = [pltpu.make_async_copy(o_ref, o_hbm, local_sems.at[0])]
     for e in range(2):
         late = c // 2
         owner = (1 - late) * (2 * c + e) + late * (7 - 2 * c - e)
         cross = lax.rem(late + y, 2)
         slot = 4 * cross + 2 * lax.rem(owner + c, 2) + lax.rem(owner // 2 + c // 2, 2)
-        kc_ref[e * chunk_len:(e + 1) * chunk_len] = kv_buf[slot, cross, 0]
-        vc_ref[e * chunk_len:(e + 1) * chunk_len] = kv_buf[slot, cross, 1]
+        sl = pl.ds(e * chunk_len, chunk_len)
+        stores.append(pltpu.make_async_copy(kv_buf.at[slot, cross, 0], kc_ref.at[sl, :], local_sems.at[1 + 2 * e]))
+        stores.append(pltpu.make_async_copy(kv_buf.at[slot, cross, 1], vc_ref.at[sl, :], local_sems.at[2 + 2 * e]))
+    for store in stores[::-1]:
+        store.start()
 
     weights_arrived((3,), 2)
     weights_arrived((3,), 3)
+    for store in stores:
+        store.wait()
     for hd in range(2):
         for n in range(7):
             kv_copy(n, hd).wait_send()
@@ -430,8 +443,8 @@
     n = N_EARLY + 1
     return pl.pallas_call(
         attention_kernel,
-        in_specs=[vm] * 6 + [hbm] * 4,
-        out_specs=[vm, vm, vm, hbm, hbm, hbm, hbm],
+        in_specs=[hbm, vm, vm] + [hbm] * 7,
+        out_specs=[hbm] * 7,
         out_shape=[
             jax.ShapeDtypeStruct((2, rows, width), bf16),
             jax.ShapeDtypeStruct((2 * rows, 128), bf16),
@@ -442,6 +455,12 @@
             jax.ShapeDtypeStruct((N_CHUNKS - 1, 4, TILE, dim), bf16),
         ],
         scratch_shapes=[
+            pltpu.VMEM((rows, dim), bf16),
+            pltpu.VMEM(wq.shape, bf16),
+            pltpu.VMEM(wk.shape, bf16),
+            pltpu.VMEM(wv.shape, bf16),
+            pltpu.VMEM((2, rows, width), bf16),
+            pltpu.SemaphoreType.DMA((5,)),
             pltpu.VMEM((rows, 128), jnp.float32),
             pltpu.VMEM((rows, 128), jnp.float32),
             pltpu.VMEM((rows, dim), bf16),
@@ -466,7 +485,7 @@
     )(x, gain, freq, wq, wk, wv, wo, w1, w3, w2)
 
 
-M_BLOCK = 512
+M_BLOCK = 1024
 LATE_FORWARD = {3: (5,), 7: (6,), 11: (7,)}
 LATE_SECOND = {3: (4,), 8: (5,), 12: (6,)}
 END_SECOND = {15: (7,)}
@@ -474,8 +493,8 @@
 STEPS = 2 * N_CHUNKS - 1
 
 
-def mlp_kernel(x_ref, gain_ref, o_ref, wo_ref, ro_ref, w1_ref, w3_ref, w2_ref, a1_ref, a3_ref, a2_ref, out_ref, hid_ref, r1_ref, r3_ref, r2_ref, e1_ref, e3_ref, e2_ref,
-               w1_sc, w3_sc, w2_sc, b_ref, acc_sc, hid_sc, load_sems, store_sems, send_sems, recv_sems):
+def mlp_kernel(x_hbm, gain_ref, o_hbm, wo_hbm, ro_hbm, w1_ref, w3_ref, w2_ref, a1_ref, a3_ref, a2_ref, out_ref, hid_ref, r1_ref, r3_ref, r2_ref, e1_ref, e3_ref, e2_ref,
+               w1_sc, w3_sc, w2_sc, x_ref, o_ref, wo_ref, ro_ref, first_sems, b_ref, acc_sc, hid_sc, load_sems, store_sems, send_sems, recv_sems):
     dim = x_ref.shape[1]
     width = 4 * TILE
     n_tiles = w1_ref.shape[1] // TILE
@@ -522,6 +541,9 @@
 
         lax.fori_loop(0, b_ref.shape[0] // M_BLOCK, rows_step, 0)
 
+    firsts = [pltpu.make_async_copy(*pair, first_sems.at[n]) for n, pair in enumerate(((wo_hbm, wo_ref), (ro_hbm, ro_ref), (o_hbm, o_ref), (x_hbm, x_ref)))]
+    for first in firsts:
+        first.start()
     net.barrier()
     net.start(0, N_EARLY, slice(PART, 3))
     net.start(0, N_EARLY + 1)
@@ -540,6 +562,8 @@
         b_ref[sl, :] = normed_rows(residual, gain_ref[...].astype(jnp.float32)[None, :])
         return carry
 
+    for first in firsts:
+        first.wait()
     lax.fori_loop(0, x_ref.shape[0] // Q_ROWS, residual_rows, 0)
     lane_tile = lax.broadcasted_iota(jnp.int32, (1, width), 1) // TILE
 
@@ -656,7 +680,7 @@
     n = N_CHUNKS
     return pl.pallas_call(
         mlp_kernel,
-        in_specs=[vm] * 5 + [hbm] * 6,
+        in_specs=[hbm, vm] + [hbm] * 9,
         out_specs=[hbm] * 8,
         out_shape=[jax.ShapeDtypeStruct((rows, dim), jnp.float32), jax.ShapeDtypeStruct((rows, left), bf16)] + [jax.ShapeDtypeStruct(a.shape, bf16) for a in early] + [jax.ShapeDtypeStruct(s, bf16) for s in ((dim, left), (dim, left), (left, dim))],
         input_output_aliases={8: 2, 9: 3, 10: 4},
@@ -664,6 +688,11 @@
             pltpu.VMEM((2, dim, width), bf16),
             pltpu.VMEM((2, dim, width), bf16),
             pltpu.VMEM((2, width, dim), bf16),
+            pltpu.VMEM(x.shape, bf16),
+            pltpu.VMEM(o.shape, bf16),
+            pltpu.VMEM(wo.shape, bf16),
+            pltpu.VMEM(ro.shape, bf16),
+            pltpu.SemaphoreType.DMA((4,)),
             pltpu.VMEM((rows, dim), bf16),
             pltpu.VMEM((rows, dim), jnp.float32),
             pltpu.VMEM((rows, left), bf16),
@@ -686,7 +715,7 @@
 
 def last_product(total, hidden, w2, k_cache, v_cache):
     rows, dim = total.shape
-    steps = rows // Q_ROWS
+    steps = rows // 128
 
     def by_rows(a):
         return pl.BlockSpec((a.shape[0] // steps, a.shape[1]), lambda i: (i, 0))

time: 330 us -> 325 us (0.985)
  Pallas kernels: 329 us -> 323 us
    pallas_call x2, Pallas kernels: 322 us -> 314 us  [the longest x1 191 us: attention(): pl.pallas_call(attention_kernel, in_specs=[hbm, vm, vm] + [hbm] * 7, out_...]
where the time goes in v7:
time: 325 us; the launch traced here: 324 us
  Pallas kernels  323 us (99%)
    pallas_call x1, Pallas kernels, attention(): pl.pallas_call(attention_kernel, in_specs=[hbm, vm, vm] + [hbm] * 7, out_...  191 us
    pallas_call x1, Pallas kernels, mlp(): pl.pallas_call(mlp_kernel, in_specs=[hbm, vm] + [hbm] * 9, out_specs=[hbm...  123 us
    pallas_call x1, Pallas kernels, last_product(): pl.pallas_call(last_kernel, grid=(steps,), in_specs=[by_rows(total), by_r...  9.08 us

profile of v7, /device:TPU:5, one launch (start us, length us, event | category | flops | bytes accessed | tf_op | source)
XLA Modules:
  0.0 324.3 jit_solution(11097830255732124166)
XLA Ops:
  0.6 0.5 fusion.2.freq_ref
  1.2 191.1 %attention.1 = (bf16[2,1024,768]{2,1,0:T(8,128)(2,1)}, bf16[2048,128]{1,0:T(8,128)(2,1)}, bf16[2048,128]{1,0:T(8,128)(2,1)}, bf16[768,1536]{1,0:T(8,128)(2,1)}, ...) custom-call(bf16[1024,1536]{1,0:T(8,128)(2,1)} %x_hbm.3, ...), custom_call_target="tpu_custom_call" | custom-call | flops 51539607552 | bytes 33554432 | tf_op jit(solution)/shard_map/attention/pallas_call | solution.py:444
  192.3 123.0 %mlp.1 = (f32[1024,1536]{1,0:T(8,128)}, bf16[1024,384]{1,0:T(8,128)(2,1)}, bf16[8,4,384,512]{3,2,1,0:T(8,128)(2,1)}, bf16[8,4,384,512]{3,2,1,0:T(8,128)(2,1)}, b...) custom-call(bf16[1024,1536]{1,0:T(8,128)(2,1)} %x_hbm.3, ...), custom_call_target="tpu_custom_call", output_to_operand_aliasing={{2}: (8, {}), {3}: (9, {}), {4}: (10, {})} | custom-call | flops 84557168640 | bytes 82575360 | tf_op jit(solution)/shard_map/mlp/pallas_call | solution.py:681
  315.2 9.1 %last_product.1 = (bf16[1024,1536]{1,0:T(8,128)(2,1)}, bf16[2048,128]{1,0:T(8,128)(2,1)}, bf16[2048,128]{1,0:T(8,128)(2,1)}) custom-call(f32[1024,1536]{1,0:T(8,128)} %get-tuple-element.18.sum_ref, bf16[1024,384]{1,0:T(8,128)(2,1)} %get-tuple-element.19.hid_ref, bf16[384,1536]{1,0:T(8,128)(2,1)} %get-tuple-element.20.w2_ref, ...), custom_call_target="tpu_custom_call" | custom-call | flops 1207959552 | bytes 9437184 | tf_op jit(solution)/shard_map/last_product/pallas_call | solution.py:724

commit v8 on v7

--- a/solution.py
+++ b/solution.py
@@ -715,7 +715,7 @@
 
 def last_product(total, hidden, w2, k_cache, v_cache):
     rows, dim = total.shape
-    steps = rows // 128
+    steps = rows // 512
 
     def by_rows(a):
         return pl.BlockSpec((a.shape[0] // steps, a.shape[1]), lambda i: (i, 0))

time: 325 us -> 322 us (level)
  no operation moved by 1% of the time
where the time goes in v8:
time: 322 us; the launch traced here: 321 us
  Pallas kernels  320 us (99%)
    pallas_call x1, Pallas kernels, attention(): pl.pallas_call(attention_kernel, in_specs=[hbm, vm, vm] + [hbm] * 7, out_...  191 us
    pallas_call x1, Pallas kernels, mlp(): pl.pallas_call(mlp_kernel, in_specs=[hbm, vm] + [hbm] * 9, out_specs=[hbm...  123 us

profile of v8, /device:TPU:5, one launch (start us, length us, event | category | flops | bytes accessed | tf_op | source)
XLA Modules:
  0.0 321.4 jit_solution(7548725115259002575)
XLA Ops:
  0.6 0.5 fusion.2.freq_ref
  1.2 191.1 %attention.1 = (bf16[2,1024,768]{2,1,0:T(8,128)(2,1)}, bf16[2048,128]{1,0:T(8,128)(2,1)}, bf16[2048,128]{1,0:T(8,128)(2,1)}, bf16[768,1536]{1,0:T(8,128)(2,1)}, ...) custom-call(bf16[1024,1536]{1,0:T(8,128)(2,1)} %x_hbm.3, ...), custom_call_target="tpu_custom_call" | custom-call | flops 51539607552 | bytes 33554432 | tf_op jit(solution)/shard_map/attention/pallas_call | solution.py:444
  192.3 123.1 %mlp.1 = (f32[1024,1536]{1,0:T(8,128)}, bf16[1024,384]{1,0:T(8,128)(2,1)}, bf16[8,4,384,512]{3,2,1,0:T(8,128)(2,1)}, bf16[8,4,384,512]{3,2,1,0:T(8,128)(2,1)}, b...) custom-call(bf16[1024,1536]{1,0:T(8,128)(2,1)} %x_hbm.3, ...), custom_call_target="tpu_custom_call", output_to_operand_aliasing={{2}: (8, {}), {3}: (9, {}), {4}: (10, {})} | custom-call | flops 84557168640 | bytes 82575360 | tf_op jit(solution)/shard_map/mlp/pallas_call | solution.py:681
  315.4 5.9 %last_product.1 = (bf16[1024,1536]{1,0:T(8,128)(2,1)}, bf16[2048,128]{1,0:T(8,128)(2,1)}, bf16[2048,128]{1,0:T(8,128)(2,1)}) custom-call(f32[1024,1536]{1,0:T(8,128)} %get-tuple-element.18.sum_ref, bf16[1024,384]{1,0:T(8,128)(2,1)} %get-tuple-element.19.hid_ref, bf16[384,1536]{1,0:T(8,128)(2,1)} %get-tuple-element.20.w2_ref, ...), custom_call_target="tpu_custom_call" | custom-call | flops 1207959552 | bytes 9437184 | tf_op jit(solution)/shard_map/last_product/pallas_call | solution.py:724
